TPU v7x, 128 devices: a whole 4x4x4 slice. The times are simulated.
128 devices in a mesh: row: 8 (over x, core), col: 16 (over z, y).
Axes of the slice: x: 4, y: 4, z: 4, core: 2. Of those that a mesh axis runs over, the one named last changes fastest.
Arguments:
- voltage: float32 [1024, 4096], P('row', 'col'), may hold values from -6 to 6
- currents: float32 [2, 1024, 4096], P(None, 'row', 'col'), may hold values from -6 to 6
- resistance: float32 [2, 1024, 4096], P(None, 'row', 'col'), may hold values from 0.05 to 0.5
- inverse_cap: float32 [1024, 4096], P('row', 'col'), may hold values from 0.05 to 0.5
- shunt_conductance: float32 [1024, 4096], P('row', 'col'), may hold values from 0.1 to 1
- tap_index: int32 [1024, 4096], P('row', 'col'), may hold values from 0 to 8
- pad_mask: int32 [1024, 4096], P('row', 'col'), may hold values 0 or 1
- waveforms: float32 [2, 8], replicated, may hold values from -8 to 8
- k_window: bfloat16 [2, 33, 33], replicated, may hold values from -0.1 to 0.4
Outputs:
- voltage_out: float32 [1024, 4096], P('row', 'col')
- current_out: float32 [2, 1024, 4096], P(None, 'row', 'col')
All inputs are finite; a program needn't handle non-finite values. No bound on the sum of `pad_mask` on one device may be relied on, other than what follows from the above.
Results may differ from a plain program's by a relative error of at most 0.0023.
Values may be sent and summed in bfloat16 or wider, within the bound.
A program may use at most 64 MiB of HBM per device.

v0:
```python
import jax
import jax.numpy as jnp
from jax import lax
from jax.sharding import PartitionSpec as P

HALF = 16
STEPS = 2
NW = 8


def passed_along(value, axis, steps):
    count = lax.axis_size(axis)
    first, last = (max(0, -steps), min(count, count - steps))
    return lax.ppermute(value, axis, [(source, source + steps) for source in range(first, last)])


def with_halo(value, sides, width):
    for axis, dim in sides:
        devices, length = (lax.axis_size(axis), value.shape[dim])
        up = [(i, (i + 1) % devices) for i in range(devices - 1)]
        down = [(j, i) for i, j in up]
        last = lax.slice_in_dim(value, length - width, length, axis=dim)
        first = lax.slice_in_dim(value, 0, width, axis=dim)
        before = lax.ppermute(last, axis, up)
        after = lax.ppermute(first, axis, down)
        value = jnp.concatenate([before, value, after], axis=dim)
    return value


def toeplitz_rows(kernel_row, width_in, width_out):
    window_span = kernel_row.shape[1]
    in_index = jnp.arange(width_in, dtype=jnp.int32)[:, None]
    out_index = jnp.arange(width_out, dtype=jnp.int32)[None, :]
    offsets_col = in_index - out_index
    inside = (offsets_col >= 0) & (offsets_col < window_span)
    entries = jnp.take(kernel_row, jnp.clip(offsets_col, 0, window_span - 1), axis=1)
    return jnp.where(inside[None], entries, jnp.zeros_like(entries))


def block_width():
    return 128


def banded_tables(kernel):
    window_span = kernel.shape[1]
    width = block_width()
    flat_rows = kernel.reshape(2 * window_span, window_span)
    tables = toeplitz_rows(flat_rows, width + window_span - 1, width)
    return tables.reshape(2, window_span, width + window_span - 1, width)


def window_apply(padded, tables, row_count, col_count):
    window_span = tables.shape[1]
    width = tables.shape[3]
    margin = window_span - 1
    groups = col_count // width

    def accumulate(offset, running):
        row_slab = lax.dynamic_slice_in_dim(padded, offset, row_count, 1)
        matrix = lax.dynamic_index_in_dim(tables, offset, 1, keepdims=False)
        leading = row_slab[:, :, :col_count].reshape(2, row_count, groups, width)
        trailing = row_slab[:, :, width:col_count].reshape(2, row_count, groups - 1, width)
        last_tail = row_slab[:, :, col_count:][:, :, None, :]
        tails = jnp.concatenate([trailing[:, :, :, :margin], last_tail], axis=2)
        windows = jnp.concatenate([leading, tails], axis=3)
        product = jnp.einsum("crnj,cjk->crnk", windows, matrix, preferred_element_type=jnp.float32)
        return running + product.reshape(2, row_count, col_count)

    start = jnp.zeros((2, row_count, col_count), jnp.float32)
    return lax.fori_loop(0, window_span, accumulate, start)


def loads_of(tap_index, wave_row):
    running = jnp.zeros(tap_index.shape, jnp.float32)
    for which in range(NW):
        running = running + jnp.where(tap_index == which, wave_row[which], jnp.float32(0.0))
    return running


def local(
    voltage,
    currents,
    resistance,
    inverse_cap,
    shunt_conductance,
    tap_index,
    pad_mask,
    waveforms,
    k_window,
):
    row_count, col_count = voltage.shape
    tables = banded_tables(k_window)
    for step_index in range(STEPS):
        next_rows = passed_along(voltage[:1, :], "row", -1)
        next_cols = passed_along(voltage[:, :1], "col", -1)
        below = jnp.concatenate([voltage[1:, :], next_rows], axis=0)
        beside = jnp.concatenate([voltage[:, 1:], next_cols], axis=1)
        drop_pair = jnp.stack([voltage - below, voltage - beside])
        driving = (drop_pair - resistance * currents).astype(jnp.bfloat16)
        padded = with_halo(driving, (("row", 1), ("col", 2)), HALF)
        currents = currents + window_apply(padded, tables, row_count, col_count)
        upper = passed_along(currents[0, -1:, :], "row", 1)
        leftward = passed_along(currents[1, :, -1:], "col", 1)
        before_x = jnp.concatenate([upper, currents[0, :-1, :]], axis=0)
        before_y = jnp.concatenate([leftward, currents[1, :, :-1]], axis=1)
        divergence = currents[0] - before_x + currents[1] - before_y
        load = loads_of(tap_index, waveforms[step_index])
        voltage = voltage + inverse_cap * (load - divergence - shunt_conductance * voltage)
        voltage = jnp.where(pad_mask == 1, jnp.float32(0.0), voltage)
    return (voltage, currents)


def solution(mesh):
    placed = (
        P("row", "col"),
        P(None, "row", "col"),
        P(None, "row", "col"),
        P("row", "col"),
        P("row", "col"),
        P("row", "col"),
        P("row", "col"),
        P(),
        P(),
    )
    return jax.shard_map(
        local,
        mesh=mesh,
        in_specs=placed,
        out_specs=(P("row", "col"), P(None, "row", "col")),
        check_vma=False,
    )
```

profile of v0, /device:TPU:20, one launch (start us, length us, event | category | flops | bytes accessed | tf_op | source)
XLA Modules:
  0.0 270.6 jit_solution(17846719390119896086)
XLA Ops:
  1.6 2.4 collective-permute-start.1
  4.8 1.9 collective-permute-start
  10.1 72.1 %gather_fusion = bf16[20480,66]{1,0:T(8,128)(2,1)} fusion(bf16[66,33]{0,1:T(8,128)(2,1)S(1)} %reshape.140, s32[20480]{0:T(1024)S(1)} %fusion.43), kind=kCustom, calls=%fused_computation | custom fusion | bytes 5488640 | tf_op jit(solution)/shard_map/jit(_take)/gather | solution.py:36
  82.3 7.2 %copy.38 = bf16[160,128,66]{1,0,2:T(8,128)(2,1)} copy(bf16[160,128,66]{2,1,0:T(8,128)(2,1)} %bitcast.146) | data formatting | bytes 5406720 | tf_op jit(solution)/shard_map/jit(_take)/gather | solution.py:36
  89.7 2.4 collective-permute-start.2
  92.2 3.2 %collective-permute-start.3 = (bf16[2,16,256]{1,2,0:T(8,128)(2,1)S(1)}, bf16[2,16,256]{1,2,0:T(8,128)(2,1)S(1)}, u32[]{:S(2)}, u32[]{:S(2)}) collective-permute-start(bf16[2,16,256]{1,2,0:T(8,128)(2,1)S(1)} %get-tuple-element.239), channel_id=1, source_target_pairs={{16,0},{32,16},{48,32},{64,48},{80,64},{96,80},{112,96},{17,1},{33... | collective-permute-start | bytes 49160 | tf_op jit(solution)/shard_map/ppermute | solution.py:25
  95.3 2.1 select_select_fusion
  97.9 3.5 %collective-permute-start.4 = (bf16[2,160,16]{1,2,0:T(8,128)(2,1)S(1)}, bf16[2,160,16]{1,2,0:T(8,128)(2,1)S(1)}, u32[]{:S(2)}, u32[]{:S(2)}) collective-permute-start(bf16[2,160,16]{1,2,0:T(8,128)(2,1)S(1)} %get-tuple-element.230), channel_id=1, source_target_pairs={{0,1},{1,2},{2,3},{3,4},{4,5},{5,6},{6,7},{7,8},{8,9},{9,10},{10,1... | collective-permute-start | bytes 30728 | tf_op jit(solution)/shard_map/ppermute | solution.py:24
  101.4 2.4 collective-permute-start.5
  104.5 1.9 copy.39
  106.4 2.0 collective-permute-done.5
  108.7 51.1 %while.28 = (s32[]{:T(128)}, f32[2,128,256]{1,2,0:T(8,128)S(1)}, bf16[2,160,288]{1,2,0:T(8,128)(2,1)S(1)}, bf16[2,33,160,128]{3,2,0,1:T(8,128)(2,1)}, s32[]{:T(128)}, /*index=5*/s32[]{:T(128)}, s32[]{}, s32[]{}) while((s32[]{:T(128)}, f32[2,128,256]{1,2,0:T(8,128)S(1)}, bf16[2,160,288]{1,2,0:T(8,128)(2,1)S(1)}, ...), condition=%wide.region_1.2_spmd.clone, body=%wide.region_0.1_spmd.clone.sunk | while | flops 21594116 | bytes 1753739 | solution.py:70
  109.0 1.1 fusion.62
  110.6 1.1 fusion.62
  112.1 1.1 fusion.62
  113.7 1.1 fusion.62
  115.2 1.1 fusion.62
  116.8 1.1 fusion.62
  118.3 1.1 fusion.62
  119.9 1.1 fusion.62
  121.4 1.1 fusion.62
  123.0 1.1 fusion.62
  124.5 1.1 fusion.62
  126.1 1.1 fusion.62
  127.6 1.1 fusion.62
  129.2 1.1 fusion.62
  130.7 1.1 fusion.62
  132.3 1.1 fusion.62
  133.8 1.1 fusion.62
  135.4 1.1 fusion.62
  136.9 1.1 fusion.62
  138.5 1.1 fusion.62
  140.0 1.1 fusion.62
  141.6 1.1 fusion.62
  143.1 1.1 fusion.62
  144.7 1.1 fusion.62
  146.2 1.1 fusion.62
  157.1 1.1 fusion.62
  160.2 6.0 %collective-permute-start.7 = (f32[128,1]{0,1:T(1,128)S(1)}, f32[128,1]{0,1:T(1,128)S(1)}, u32[]{:S(2)}, u32[]{:S(2)}) collective-permute-start(f32[128,1]{0,1:T(1,128)S(1)} %bitcast.150), channel_id=1, source_target_pairs={{0,1},{1,2},{2,3},{3,4},{4,5},{5,6},{6,7},{7,8},{8,9},{9,10},{10,1... | collective-permute-start | bytes 1544 | tf_op jit(solution)/shard_map/ppermute | solution.py:14
  166.3 1.9 collective-permute-start.6
  168.3 2.8 %collective-permute-done.6 = f32[1,256]{1,0:T(1,128)S(1)} collective-permute-done((f32[1,256]{1,0:T(1,128)S(1)}, f32[1,256]{1,0:T(1,128)S(1)}, u32[]{:S(2)}, u32[]{:S(2)}) %collective-permute-start.6) | collective-permute-done | bytes 1056 | tf_op jit(solution)/shard_map/ppermute | solution.py:14
  171.2 5.4 %fusion.36 = (f32[128,256]{1,0:T(8,128)S(1)}, pred[128,256]{1,0:T(8,128)(4,1)S(1)}, pred[128,256]{1,0:T(8,128)(4,1)S(1)}, pred[128,256]{1,0:T(8,128)(4,1)S(1)}, ...) fusion(f32[128,256]{1,0:T(8,128)S(1)} %copy-done.3, ...), kind=kLoop, calls=%fused_computation.61 | loop fusion | flops 1146880 | bytes 1605664 | tf_op jit(solution)/shard_map/jit(_where)/select_n | solution.py:109
  176.6 1.9 collective-permute-start.8
  178.5 1.9 collective-permute-start.9
  180.6 4.3 %collective-permute-done.9 = f32[128,1]{1,0:T(8,128)S(1)} collective-permute-done((f32[128,1]{1,0:T(8,128)S(1)}, f32[128,1]{1,0:T(8,128)S(1)}, u32[]{:S(2)}, u32[]{:S(2)}) %collective-permute-start.9) | collective-permute-done | bytes 544 | tf_op jit(solution)/shard_map/ppermute | solution.py:14
  185.1 1.9 collective-permute-start.10
  187.0 3.6 %collective-permute-start.11 = (bf16[2,16,256]{2,1,0:T(8,128)(2,1)S(1)}, bf16[2,16,256]{2,1,0:T(8,128)(2,1)S(1)}, u32[]{:S(2)}, u32[]{:S(2)}) collective-permute-start(bf16[2,16,256]{2,1,0:T(8,128)(2,1)S(1)} %get-tuple-element.235), channel_id=1, source_target_pairs={{16,0},{32,16},{48,32},{64,48},{80,64},{96,80},{112,96},{17,1},{33... | collective-permute-start | bytes 49160 | tf_op jit(solution)/shard_map/ppermute | solution.py:25
  190.7 1.4 collective-permute-done.11
  192.2 4.9 %collective-permute-start.12 = (bf16[2,160,16]{2,1,0:T(8,128)(2,1)S(1)}, bf16[2,160,16]{2,1,0:T(8,128)(2,1)S(1)}, u32[]{:S(2)}, u32[]{:S(2)}) collective-permute-start(bf16[2,160,16]{2,1,0:T(8,128)(2,1)S(1)} %get-tuple-element.232), channel_id=1, source_target_pairs={{0,1},{1,2},{2,3},{3,4},{4,5},{5,6},{6,7},{7,8},{8,9},{9,10},{10,1... | collective-permute-start | bytes 30728 | tf_op jit(solution)/shard_map/ppermute | solution.py:24
  197.2 1.9 collective-permute-start.13
  199.7 4.7 %collective-permute-done.13 = bf16[2,160,16]{2,1,0:T(8,128)(2,1)S(1)} collective-permute-done((bf16[2,160,16]{2,1,0:T(8,128)(2,1)S(1)}, bf16[2,160,16]{2,1,0:T(8,128)(2,1)S(1)}, u32[]{:S(2)}, u32[]{:S(2)}) %collective-permute-start.13) | collective-permute-done | bytes 10272 | tf_op jit(solution)/shard_map/ppermute | solution.py:25
  204.7 51.1 %while.29 = (s32[]{:T(128)}, f32[2,128,256]{1,2,0:T(8,128)S(1)}, bf16[2,160,288]{1,2,0:T(8,128)(2,1)S(1)}, bf16[2,33,160,128]{3,2,0,1:T(8,128)(2,1)}, s32[]{:T(128)}, /*index=5*/s32[]{:T(128)}, s32[]{}, s32[]{}) while((s32[]{:T(128)}, f32[2,128,256]{1,2,0:T(8,128)S(1)}, bf16[2,160,288]{1,2,0:T(8,128)(2,1)S(1)}, ...), condition=%wide.region_3.4_spmd.clone, body=%wide.region_2.3_spmd.clone.sunk | while | flops 21594116 | bytes 1753739 | solution.py:70
  212.8 1.1 fusion.65
  217.4 1.1 fusion.65
  222.1 1.1 fusion.65
  232.9 1.1 fusion.65
  237.6 1.1 fusion.65
  242.2 1.1 fusion.65
  246.9 1.1 fusion.65
  251.5 1.1 fusion.65
  256.2 3.8 %collective-permute-start.15 = (f32[128,1]{0,1:T(1,128)S(1)}, f32[128,1]{0,1:T(1,128)S(1)}, u32[]{:S(2)}, u32[]{:S(2)}) collective-permute-start(f32[128,1]{0,1:T(1,128)S(1)} %bitcast.151), channel_id=1, source_target_pairs={{0,1},{1,2},{2,3},{3,4},{4,5},{5,6},{6,7},{7,8},{8,9},{9,10},{10,1... | collective-permute-start | bytes 1544 | tf_op jit(solution)/shard_map/ppermute | solution.py:14
  260.0 1.9 collective-permute-start.14
  262.0 2.8 %collective-permute-done.14 = f32[1,256]{1,0:T(1,128)S(1)} collective-permute-done((f32[1,256]{1,0:T(1,128)S(1)}, f32[1,256]{1,0:T(1,128)S(1)}, u32[]{:S(2)}, u32[]{:S(2)}) %collective-permute-start.14) | collective-permute-done | bytes 1056 | tf_op jit(solution)/shard_map/ppermute | solution.py:14
  264.9 5.7 %fusion.28 = f32[128,256]{1,0:T(8,128)} fusion(pred[128,256]{1,0:T(8,128)(4,1)S(1)} %get-tuple-element.229, f32[128,256]{1,0:T(8,128)S(1)} %get-tuple-element.220, f32[128,256]{1,0:T(8,128)S(1)} %copy-done.4, f32[2,128,256]{2,1,0:T(8,128)S(1)} %add.163, f32[127,256]{1,0:T(8,128)S(1)} %slice_bitcast_fusion.4, f32[1,256]{1,0:T(1,128)S(1)} %collective-permute-done.14, ...), kind=kLoop, calls=%fused_computation.49 | loop fusion | flops 851968 | bytes 1343520 | tf_op jit(solution)/shard_map/jit(_where)/select_n | solution.py:109
  (435 shorter events, 70.3 us)
Async XLA Ops:
  1.6 87.8 %collective-permute-start.1 = (f32[128,1]{0,1:T(1,128)S(1)}, f32[128,1]{0,1:T(1,128)S(1)}, u32[]{:S(2)}, u32[]{:S(2)}) collective-permute-start(f32[128,1]{0,1:T(1,128)S(1)} %slice.280), channel_id=1, source_target_pairs={{1,0},{2,1},{3,2},{4,3},{5,4},{6,5},{7,6},{8,7},{9,8},{10,9},{11,1... | collective-permute-start | bytes 1544 | tf_op jit(solution)/shard_map/ppermute | solution.py:14
  4.8 84.6 %collective-permute-start = (f32[1,256]{0,1:T(8,128)S(1)}, f32[1,256]{0,1:T(8,128)S(1)}, u32[]{:S(2)}, u32[]{:S(2)}) collective-permute-start(f32[1,256]{0,1:T(8,128)S(1)} %copy.30), channel_id=1, source_target_pairs={{16,0},{32,16},{48,32},{64,48},{80,64},{96,80},{112,96},{17,1},{33... | collective-permute-start | bytes 3080 | tf_op jit(solution)/shard_map/ppermute | solution.py:14
  89.7 7.7 %collective-permute-start.2 = (bf16[2,16,256]{1,2,0:T(8,128)(2,1)S(1)}, bf16[2,16,256]{1,2,0:T(8,128)(2,1)S(1)}, u32[]{:S(2)}, u32[]{:S(2)}) collective-permute-start(bf16[2,16,256]{1,2,0:T(8,128)(2,1)S(1)} %get-tuple-element.238), channel_id=1, source_target_pairs={{0,16},{16,32},{32,48},{48,64},{64,80},{80,96},{96,112},{1,17},{17... | collective-permute-start | bytes 49160 | tf_op jit(solution)/shard_map/ppermute | solution.py:24
  92.2 5.7 %collective-permute-start.3 = (bf16[2,16,256]{1,2,0:T(8,128)(2,1)S(1)}, bf16[2,16,256]{1,2,0:T(8,128)(2,1)S(1)}, u32[]{:S(2)}, u32[]{:S(2)}) collective-permute-start(bf16[2,16,256]{1,2,0:T(8,128)(2,1)S(1)} %get-tuple-element.239), channel_id=1, source_target_pairs={{16,0},{32,16},{48,32},{64,48},{80,64},{96,80},{112,96},{17,1},{33... | collective-permute-start | bytes 49160 | tf_op jit(solution)/shard_map/ppermute | solution.py:25
  95.3 8.4 %copy-start.8 = (f32[2,8]{1,0:T(2,128)S(1)}, f32[2,8]{1,0:T(2,128)}, u32[]{:S(2)}) copy-start(f32[2,8]{1,0:T(2,128)} %param.20) | copy-start | bytes 196
  97.9 8.5 %collective-permute-start.4 = (bf16[2,160,16]{1,2,0:T(8,128)(2,1)S(1)}, bf16[2,160,16]{1,2,0:T(8,128)(2,1)S(1)}, u32[]{:S(2)}, u32[]{:S(2)}) collective-permute-start(bf16[2,160,16]{1,2,0:T(8,128)(2,1)S(1)} %get-tuple-element.230), channel_id=1, source_target_pairs={{0,1},{1,2},{2,3},{3,4},{4,5},{5,6},{6,7},{7,8},{8,9},{9,10},{10,1... | collective-permute-start | bytes 30728 | tf_op jit(solution)/shard_map/ppermute | solution.py:24
  101.4 7.0 %collective-permute-start.5 = (bf16[2,160,16]{1,2,0:T(8,128)(2,1)S(1)}, bf16[2,160,16]{1,2,0:T(8,128)(2,1)S(1)}, u32[]{:S(2)}, u32[]{:S(2)}) collective-permute-start(bf16[2,160,16]{1,2,0:T(8,128)(2,1)S(1)} %get-tuple-element.231), channel_id=1, source_target_pairs={{1,0},{2,1},{3,2},{4,3},{5,4},{6,5},{7,6},{8,7},{9,8},{10,9},{11,1... | collective-permute-start | bytes 30728 | tf_op jit(solution)/shard_map/ppermute | solution.py:25
  108.6 51.4 %copy-start.1 = (f32[2,128,256]{2,1,0:T(8,128)S(1)}, f32[2,128,256]{2,1,0:T(8,128)}, u32[]{:S(2)}) copy-start(f32[2,128,256]{2,1,0:T(8,128)} %param.14) | copy-start | bytes 786436
  108.6 62.5 %copy-start.3 = (f32[128,256]{1,0:T(8,128)S(1)}, f32[128,256]{1,0:T(8,128)}, u32[]{:S(2)}) copy-start(f32[128,256]{1,0:T(8,128)} %param.13) | copy-start | bytes 393220
  108.6 62.5 %copy-start.4 = (f32[128,256]{1,0:T(8,128)S(1)}, f32[128,256]{1,0:T(8,128)}, u32[]{:S(2)}) copy-start(f32[128,256]{1,0:T(8,128)} %param.16) | copy-start | bytes 393220
  108.6 62.5 %copy-start.5 = (f32[128,256]{1,0:T(8,128)S(1)}, f32[128,256]{1,0:T(8,128)}, u32[]{:S(2)}) copy-start(f32[128,256]{1,0:T(8,128)} %param.17) | copy-start | bytes 393220
  108.7 62.5 %copy-start.6 = (s32[128,256]{1,0:T(8,128)S(1)}, s32[128,256]{1,0:T(8,128)}, u32[]{:S(2)}) copy-start(s32[128,256]{1,0:T(8,128)} %param.18) | copy-start | bytes 393220
  108.7 62.5 %copy-start.7 = (s32[128,256]{1,0:T(8,128)S(1)}, s32[128,256]{1,0:T(8,128)}, u32[]{:S(2)}) copy-start(s32[128,256]{1,0:T(8,128)} %param.19) | copy-start | bytes 393220
  159.8 25.2 %copy-start.2 = (f32[2,128,256]{2,1,0:T(8,128)S(1)}, f32[2,128,256]{2,1,0:T(8,128)}, u32[]{:S(2)}) copy-start(f32[2,128,256]{2,1,0:T(8,128)} %param.15) | copy-start | bytes 786436
  160.2 8.0 %collective-permute-start.7 = (f32[128,1]{0,1:T(1,128)S(1)}, f32[128,1]{0,1:T(1,128)S(1)}, u32[]{:S(2)}, u32[]{:S(2)}) collective-permute-start(f32[128,1]{0,1:T(1,128)S(1)} %bitcast.150), channel_id=1, source_target_pairs={{0,1},{1,2},{2,3},{3,4},{4,5},{5,6},{6,7},{7,8},{8,9},{9,10},{10,1... | collective-permute-start | bytes 1544 | tf_op jit(solution)/shard_map/ppermute | solution.py:14
  166.3 4.9 %collective-permute-start.6 = (f32[1,256]{1,0:T(1,128)S(1)}, f32[1,256]{1,0:T(1,128)S(1)}, u32[]{:S(2)}, u32[]{:S(2)}) collective-permute-start(f32[1,256]{1,0:T(1,128)S(1)} %slice_bitcast_fusion.11), channel_id=1, source_target_pairs={{0,16},{16,32},{32,48},{48,64},{64,80},{80,96},{96,112},{1,17},{17... | collective-permute-start | bytes 3080 | tf_op jit(solution)/shard_map/ppermute | solution.py:14
  176.6 8.3 %collective-permute-start.8 = (f32[1,256]{1,0:T(1,128)S(1)}, f32[1,256]{1,0:T(1,128)S(1)}, u32[]{:S(2)}, u32[]{:S(2)}) collective-permute-start(f32[1,256]{1,0:T(1,128)S(1)} %slice.290), channel_id=1, source_target_pairs={{16,0},{32,16},{48,32},{64,48},{80,64},{96,80},{112,96},{17,1},{33... | collective-permute-start | bytes 3080 | tf_op jit(solution)/shard_map/ppermute | solution.py:14
  178.5 6.4 %collective-permute-start.9 = (f32[128,1]{1,0:T(8,128)S(1)}, f32[128,1]{1,0:T(8,128)S(1)}, u32[]{:S(2)}, u32[]{:S(2)}) collective-permute-start(f32[128,1]{1,0:T(8,128)S(1)} %slice.292), channel_id=1, source_target_pairs={{1,0},{2,1},{3,2},{4,3},{5,4},{6,5},{7,6},{8,7},{9,8},{10,9},{11,1... | collective-permute-start | bytes 1544 | tf_op jit(solution)/shard_map/ppermute | solution.py:14
  185.1 5.6 %collective-permute-start.10 = (bf16[2,16,256]{2,1,0:T(8,128)(2,1)S(1)}, bf16[2,16,256]{2,1,0:T(8,128)(2,1)S(1)}, u32[]{:S(2)}, u32[]{:S(2)}) collective-permute-start(bf16[2,16,256]{2,1,0:T(8,128)(2,1)S(1)} %get-tuple-element.234), channel_id=1, source_target_pairs={{0,16},{16,32},{32,48},{48,64},{64,80},{80,96},{96,112},{1,17},{17... | collective-permute-start | bytes 49160 | tf_op jit(solution)/shard_map/ppermute | solution.py:24
  187.0 5.1 %collective-permute-start.11 = (bf16[2,16,256]{2,1,0:T(8,128)(2,1)S(1)}, bf16[2,16,256]{2,1,0:T(8,128)(2,1)S(1)}, u32[]{:S(2)}, u32[]{:S(2)}) collective-permute-start(bf16[2,16,256]{2,1,0:T(8,128)(2,1)S(1)} %get-tuple-element.235), channel_id=1, source_target_pairs={{16,0},{32,16},{48,32},{64,48},{80,64},{96,80},{112,96},{17,1},{33... | collective-permute-start | bytes 49160 | tf_op jit(solution)/shard_map/ppermute | solution.py:25
  192.2 7.5 %collective-permute-start.12 = (bf16[2,160,16]{2,1,0:T(8,128)(2,1)S(1)}, bf16[2,160,16]{2,1,0:T(8,128)(2,1)S(1)}, u32[]{:S(2)}, u32[]{:S(2)}) collective-permute-start(bf16[2,160,16]{2,1,0:T(8,128)(2,1)S(1)} %get-tuple-element.232), channel_id=1, source_target_pairs={{0,1},{1,2},{2,3},{3,4},{4,5},{5,6},{6,7},{7,8},{8,9},{9,10},{10,1... | collective-permute-start | bytes 30728 | tf_op jit(solution)/shard_map/ppermute | solution.py:24
  197.2 7.2 %collective-permute-start.13 = (bf16[2,160,16]{2,1,0:T(8,128)(2,1)S(1)}, bf16[2,160,16]{2,1,0:T(8,128)(2,1)S(1)}, u32[]{:S(2)}, u32[]{:S(2)}) collective-permute-start(bf16[2,160,16]{2,1,0:T(8,128)(2,1)S(1)} %get-tuple-element.233), channel_id=1, source_target_pairs={{1,0},{2,1},{3,2},{4,3},{5,4},{6,5},{7,6},{8,7},{9,8},{10,9},{11,1... | collective-permute-start | bytes 30728 | tf_op jit(solution)/shard_map/ppermute | solution.py:25
  256.0 14.6 %copy-start = (f32[2,128,256]{2,1,0:T(8,128)}, f32[2,128,256]{2,1,0:T(8,128)S(1)}, u32[]{:S(2)}) copy-start(f32[2,128,256]{2,1,0:T(8,128)S(1)} %add.163) | copy-start | bytes 786436
  256.2 5.7 %collective-permute-start.15 = (f32[128,1]{0,1:T(1,128)S(1)}, f32[128,1]{0,1:T(1,128)S(1)}, u32[]{:S(2)}, u32[]{:S(2)}) collective-permute-start(f32[128,1]{0,1:T(1,128)S(1)} %bitcast.151), channel_id=1, source_target_pairs={{0,1},{1,2},{2,3},{3,4},{4,5},{5,6},{6,7},{7,8},{8,9},{9,10},{10,1... | collective-permute-start | bytes 1544 | tf_op jit(solution)/shard_map/ppermute | solution.py:14
  260.0 4.9 %collective-permute-start.14 = (f32[1,256]{1,0:T(1,128)S(1)}, f32[1,256]{1,0:T(1,128)S(1)}, u32[]{:S(2)}, u32[]{:S(2)}) collective-permute-start(f32[1,256]{1,0:T(1,128)S(1)} %slice_bitcast_fusion.10), channel_id=1, source_target_pairs={{0,16},{16,32},{32,48},{48,64},{64,80},{80,96},{96,112},{1,17},{17... | collective-permute-start | bytes 3080 | tf_op jit(solution)/shard_map/ppermute | solution.py:14
where the time goes:
time: 274 us; the launch traced here: 271 us
  local copies, waits for them, and re-layouts  110 us (40%)
  matrix products  73.4 us (27%)
  starting transfers between devices  45.6 us (17%)
  waiting for transfers between devices  19.1 us (7%)
  other arithmetic  18.3 us (7%)
  loops' own time  3.19 us (1%)
    gather x2, local copies, waits for them, and re-layouts, toeplitz_rows(): jnp.take(kernel_row, jnp.clip(offsets_col, 0, window_span - 1), axis=1)  79.3 us
    dot_general x66, matrix products, accumulate(): jnp.einsum('crnj,cjk->crnk', windows, matrix, preferred_element_type=jnp....  73.4 us
    ppermute x8, starting transfers between devices, passed_along(): lax.ppermute(value, axis, [(source, source + steps) for source in range(f...  21.7 us
    ppermute x4, starting transfers between devices, with_halo(): before = lax.ppermute(last, axis, up)  12.8 us
    ppermute x4, starting transfers between devices, with_halo(): after = lax.ppermute(first, axis, down)  11.1 us
    select_n x2, other arithmetic, local(): voltage = jnp.where(pad_mask == 1, jnp.float32(0.0), voltage)  11.1 us
    ppermute x8, waiting for transfers between devices, passed_along(): lax.ppermute(value, axis, [(source, source + steps) for source in range(f...  10 us
    ppermute x4, waiting for transfers between devices, with_halo(): after = lax.ppermute(first, axis, down)  8.53 us
  transfers between devices with their start and end apart: 16, of which 8 were waited for; matrix products, arithmetic and copies ran while one was open for 33% of the time, Pallas kernels for 0%

commit v1 on v0

v1 whole, which is shorter than its diff:
```python
import functools

import jax
import jax.numpy as jnp
from jax import lax
from jax.experimental import pallas as pl
from jax.experimental.pallas import tpu as pltpu
from jax.sharding import PartitionSpec as P

HALF = 16
SPAN = 2 * HALF + 1
STEPS = 2
NW = 8
ROWS = 128
COLS = 256
LANES = 128
TOP = 24
EXT = ROWS + 2 * TOP
DEEP = EXT + 24
GROUP = 4
TAPS = SPAN + GROUP - 1
DEPTH = TAPS * LANES
MESH = pl.DeviceIdType.MESH
F32 = jnp.float32
BF16 = jnp.bfloat16
DIRECTIONS = ((-1, 0), (1, 0), (0, -1), (0, 1), (-1, -1), (-1, 1), (1, -1), (1, 1))


def lane_of(shape):
    return lax.broadcasted_iota(jnp.int32, shape, len(shape) - 1)


def roll(value, amount):
    return pltpu.roll(value, amount % LANES, 1)


def packed(first, second, third, fourth):
    lane = lane_of(first.shape)
    return jnp.where(lane < 32, first, jnp.where(lane < 64, second, jnp.where(lane < 96, third, fourth)))


def one_if(flag):
    return jnp.where(flag, 1, 0)


def build_table(k_ref, comp, pad_ref, base_ref, table_ref):
    pad_ref[...] = jnp.zeros_like(pad_ref)
    pad_ref[8 : 8 + SPAN, 0:SPAN] = k_ref[:, comp, :].astype(F32)
    tap = lax.broadcasted_iota(jnp.int32, (LANES, LANES), 0)
    lane = lax.broadcasted_iota(jnp.int32, (LANES, LANES), 1)
    near = jnp.where(((HALF - tap) & 127) == lane, 1.0, 0.0).astype(BF16)
    far = jnp.where(((HALF + 64 - tap) & 127) == lane, 1.0, 0.0).astype(BF16)
    near = jnp.where(tap < SPAN, near, jnp.zeros_like(near))
    far = jnp.where(tap < SPAN, far, jnp.zeros_like(far))
    here = pad_ref[8:48, :].astype(BF16)
    above = pad_ref[7:47, :].astype(BF16)
    base_ref[...] = jnp.dot(here, near, preferred_element_type=F32) + jnp.dot(above, far, preferred_element_type=F32)
    inside = ((tap - (lane & 63) + HALF) & 127) < SPAN

    def one(index, carry):
        row = jnp.broadcast_to(base_ref[pl.ds(index, 1), :], (LANES, LANES))
        turned = pltpu.roll(row, 0, 1, stride=1, stride_axis=0)
        block = jnp.where(inside, turned, 0.0).astype(BF16)
        table_ref[comp, pl.ds(pl.multiple_of(index * LANES, LANES), LANES), 0:LANES] = block
        table_ref[comp, pl.ds(pl.multiple_of((index + 2) * LANES, LANES), LANES), LANES:] = block
        return carry

    lax.fori_loop(0, SPAN + 1, one, 0)
    blank = jnp.zeros((2 * LANES, LANES), BF16)
    table_ref[comp, (SPAN + 1) * LANES :, 0:LANES] = blank
    table_ref[comp, 0 : 2 * LANES, LANES:] = blank


def kernel(
    wave_hbm, k_hbm, v_hbm, c_hbm, r_hbm, cap_hbm, shunt_hbm, tap_hbm, mask_hbm,
    vout_ref, cout_ref,
    r_ref, cap_ref, shunt_ref, tap_ref, mask_ref,
    frame_ref, cur0_ref, cur1_ref, curl_ref,
    sendl_ref, sendr_ref, fromr_ref, froml_ref,
    drive_ref, lhs_ref, table_ref, pad_ref, base_ref, load_ref,
    flow0_ref, flow1_ref, flowl_ref,
    wave_ref, k_ref, load_sem, send_sem, recv_sem, cur_sem,
):
    my_row, my_col = lax.axis_index("row"), lax.axis_index("col")
    n_row, n_col = lax.axis_size("row"), lax.axis_size("col")

    def exists(dr, dc):
        row, col = my_row + dr, my_col + dc
        ok = None
        for spot, count, delta in ((row, n_row, dr), (col, n_col, dc)):
            if delta:
                here = (spot >= 0) & (spot < count)
                ok = here if ok is None else ok & here
        return ok

    loads = [
        pltpu.make_async_copy(v_hbm, frame_ref.at[0, 0, pl.ds(TOP, ROWS), :], load_sem.at[0]),
        pltpu.make_async_copy(c_hbm.at[0], cur0_ref.at[pl.ds(8, ROWS), :], load_sem.at[1]),
        pltpu.make_async_copy(c_hbm.at[1], cur1_ref, load_sem.at[2]),
        pltpu.make_async_copy(r_hbm, r_ref, load_sem.at[3]),
        pltpu.make_async_copy(cap_hbm, cap_ref, load_sem.at[4]),
        pltpu.make_async_copy(shunt_hbm, shunt_ref, load_sem.at[5]),
        pltpu.make_async_copy(tap_hbm, tap_ref, load_sem.at[6]),
        pltpu.make_async_copy(mask_hbm, mask_ref, load_sem.at[7]),
        pltpu.make_async_copy(k_hbm, k_ref, load_sem.at[8]),
        pltpu.make_async_copy(wave_hbm, wave_ref, load_sem.at[9]),
    ]
    for one in loads:
        one.start()
    barrier = pltpu.get_barrier_semaphore()
    for dr, dc in DIRECTIONS:
        @pl.when(exists(dr, dc))
        def _(dr=dr, dc=dc):
            pl.semaphore_signal(barrier, inc=1, device_id=(my_row + dr, my_col + dc), device_id_type=MESH)

    has_up, has_down, has_left, has_right = (exists(*d) for d in DIRECTIONS[:4])

    for step in range(STEPS):
        @pl.when(jnp.logical_not(has_up))
        def _(step=step):
            frame_ref[step, :, 0:TOP, :] = jnp.zeros((3, TOP, COLS), F32)
            froml_ref[step, 0:TOP, :] = jnp.zeros((TOP, LANES), F32)
            fromr_ref[step, 0:TOP, :] = jnp.zeros((TOP, LANES), F32)

        @pl.when(jnp.logical_not(has_down))
        def _(step=step):
            frame_ref[step, :, TOP + ROWS :, :] = jnp.zeros((3, TOP, COLS), F32)
            froml_ref[step, TOP + ROWS :, :] = jnp.zeros((TOP, LANES), F32)
            fromr_ref[step, TOP + ROWS :, :] = jnp.zeros((TOP, LANES), F32)

        @pl.when(jnp.logical_not(has_left))
        def _(step=step):
            froml_ref[step] = jnp.zeros((EXT, LANES), F32)

        @pl.when(jnp.logical_not(has_right))
        def _(step=step):
            fromr_ref[step] = jnp.zeros((EXT, LANES), F32)

    @pl.when(jnp.logical_not(has_up))
    def _():
        cur0_ref[0:8, :] = jnp.zeros((8, COLS), F32)

    def message(step, which):
        frame, left, right = frame_ref.at[step], sendl_ref.at[step], sendr_ref.at[step]
        to_right, to_left = froml_ref.at[step], fromr_ref.at[step]
        low, mid, high = pl.ds(0, TOP), pl.ds(TOP, ROWS), pl.ds(TOP + ROWS, TOP)
        first, last = pl.ds(0, TOP), pl.ds(ROWS - TOP, TOP)
        source, target = (
            (frame.at[:, pl.ds(TOP, TOP), :], frame.at[:, high, :]),
            (frame.at[:, pl.ds(ROWS, TOP), :], frame.at[:, low, :]),
            (left, to_left.at[mid, :]),
            (right, to_right.at[mid, :]),
            (left.at[first, :], to_left.at[high, :]),
            (right.at[first, :], to_right.at[high, :]),
            (left.at[last, :], to_left.at[low, :]),
            (right.at[last, :], to_right.at[low, :]),
        )[which]
        dr, dc = DIRECTIONS[which]
        return pltpu.make_async_remote_copy(
            src_ref=source,
            dst_ref=target,
            send_sem=send_sem.at[step, which],
            recv_sem=recv_sem.at[step, which],
            device_id=(my_row + dr, my_col + dc),
            device_id_type=MESH,
        )

    edge = pltpu.make_async_remote_copy(
        src_ref=cur0_ref.at[pl.ds(ROWS, 8), :],
        dst_ref=cur0_ref.at[pl.ds(0, 8), :],
        send_sem=cur_sem.at[0],
        recv_sem=cur_sem.at[1],
        device_id=(my_row + 1, my_col),
        device_id_type=MESH,
    )

    def fill_products(step, lo, n):
        rows = pl.ds(TOP + lo, n)
        v = frame_ref[step, 0, rows, :]
        c1 = cur1_ref[pl.ds(lo, n), :]
        w0 = r_ref[0, pl.ds(lo, n), :] * cur0_ref[pl.ds(8 + lo, n), :]
        w1 = r_ref[1, pl.ds(lo, n), :] * c1
        frame_ref[step, 1, rows, :] = w0
        frame_ref[step, 2, rows, :] = w1
        a, b = slice(0, LANES), slice(LANES, COLS)
        sendl_ref[step, pl.ds(lo, n), :] = packed(v[:, a], roll(w0[:, a], 32), roll(w1[:, a], 64), w1[:, a])
        sendr_ref[step, pl.ds(lo, n), :] = packed(roll(v[:, b], 32), roll(w0[:, b], 64), roll(w1[:, b], 96), c1[:, b])

    def send(step):
        for which, (dr, dc) in enumerate(DIRECTIONS):
            @pl.when(exists(dr, dc))
            def _(which=which):
                message(step, which).start()

    def receive(step):
        for which, (dr, dc) in enumerate(DIRECTIONS):
            @pl.when(exists(-dr, -dc))
            def _(which=which):
                message(step, which).wait_recv()

    def drain(step):
        for which, (dr, dc) in enumerate(DIRECTIONS):
            @pl.when(exists(dr, dc))
            def _(which=which):
                message(step, which).wait_send()

    def drive(step):
        lo = jnp.where(has_up, 0, TOP)
        hi = jnp.where(has_down, EXT, TOP + ROWS)
        n = 56
        for base in range(0, EXT - 8, n):
            at, nxt = pl.ds(base, n), pl.ds(base + 1, n)
            row = lax.broadcasted_iota(jnp.int32, (n, LANES), 0) + base
            lane = lane_of((n, LANES))
            inside = (row >= lo) & (row < hi)
            left, left_next = froml_ref[step, at, :], froml_ref[step, nxt, :]
            right, right_next = fromr_ref[step, at, :], fromr_ref[step, nxt, :]
            tiles = [slice(0, LANES), slice(LANES, COLS)]
            v = [roll(left, 96)] + [frame_ref[step, 0, at, t] for t in tiles] + [right]
            below = [roll(left_next, 96)] + [frame_ref[step, 0, nxt, t] for t in tiles] + [right_next]
            w0 = [roll(left, 64)] + [frame_ref[step, 1, at, t] for t in tiles] + [roll(right, 96)]
            w1 = [roll(left, 32)] + [frame_ref[step, 2, at, t] for t in tiles] + [roll(right, 64)]
            held = [inside & has_left, inside, inside, inside & has_right]
            for comp in range(2):
                out = []
                for k in range(4):
                    if comp == 0:
                        value = v[k] - below[k] - w0[k]
                    else:
                        follow = v[min(k + 1, 3)]
                        beside = roll(jnp.where(lane == 0, follow, v[k]), 127)
                        value = v[k] - beside - w1[k]
                    out.append(jnp.where(held[k], value, 0.0))
                tl, ta, tb, tr = out
                slot = 4 * comp
                drive_ref[slot, at, :] = jnp.where(lane < 96, ta, tl)
                drive_ref[slot + 1, at, :] = roll(jnp.where(lane < 32, tb, ta), 64)
                drive_ref[slot + 2, at, :] = jnp.where(lane < 96, tb, ta)
                drive_ref[slot + 3, at, :] = roll(jnp.where(lane < 32, tr, tb), 64)
                if comp == 1:
                    drive_ref[8, at, :] = roll(jnp.where(lane < 64, ta, tl), 64)

    def convolve(comp):
        slots, start, n = ((0, 1, 2, 3), 4, 40) if comp == 0 else ((4, 5, 6, 7, 8), 8, 32)
        for tap in range(TAPS):
            pieces = [drive_ref[slot, pl.ds(start + tap, n, stride=GROUP), :] for slot in slots]
            lhs_ref[:, tap * LANES : (tap + 1) * LANES] = jnp.concatenate(pieces, axis=0).astype(BF16)
        product = jnp.dot(lhs_ref[...], table_ref[comp], preferred_element_type=F32)
        low = lane_of((n, LANES)) < 64
        for t in range(GROUP):
            half = product[:, (t // 2) * LANES : (t // 2 + 1) * LANES]
            part = [half[i * n : (i + 1) * n] for i in range(len(slots))]
            for p in range(2):
                even, odd = part[2 * p], part[2 * p + 1]
                if t % 2 == 0:
                    tile = jnp.where(low, even, roll(odd, 64))
                else:
                    tile = jnp.where(low, roll(even, 64), odd)
                cols = slice(p * LANES, (p + 1) * LANES)
                if comp == 0:
                    flow0_ref[p, pl.ds(4 + t, n, stride=GROUP), :] = tile
                else:
                    flow1_ref[p, pl.ds(t, n, stride=GROUP), :] = tile
            if comp == 1:
                flowl_ref[pl.ds(t, n, stride=GROUP), :] = roll(part[4], 64) if t % 2 == 0 else part[4]

    def advance(step):
        for p in range(2):
            cols = slice(p * LANES, (p + 1) * LANES)
            head = cur0_ref[0:8, cols] + flow0_ref[p, 0:8, :]
            cur0_ref[0:8, cols] = jnp.where(has_up, head, 0.0)
        n = 32
        for lo in range(0, ROWS, n):
            rows = pl.ds(lo, n)
            for p in range(2):
                cols = slice(p * LANES, (p + 1) * LANES)
                cur0_ref[pl.ds(8 + lo, n), cols] = cur0_ref[pl.ds(8 + lo, n), cols] + flow0_ref[p, pl.ds(8 + lo, n), :]
                cur1_ref[rows, cols] = cur1_ref[rows, cols] + flow1_ref[p, rows, :]
            curl_ref[rows, :] = jnp.where(has_left, curl_ref[rows, :] + flowl_ref[rows, :], 0.0)

    def update(step, target):
        n = 32
        for lo in range(0, ROWS, n):
            rows = pl.ds(lo, n)
            lane = lane_of((n, LANES))
            c1 = [curl_ref[rows, :], cur1_ref[rows, 0:LANES], cur1_ref[rows, LANES:]]
            for p in range(2):
                cols = slice(p * LANES, (p + 1) * LANES)
                c0 = cur0_ref[pl.ds(8 + lo, n), cols]
                before_x = cur0_ref[pl.ds(7 + lo, n), cols]
                before_y = roll(jnp.where(lane == LANES - 1, c1[p], c1[p + 1]), 1)
                divergence = c0 - before_x + c1[p + 1] - before_y
                v = frame_ref[step, 0, pl.ds(TOP + lo, n), cols]
                new = v + cap_ref[rows, cols] * (load_ref[step, rows, cols] - divergence - shunt_ref[rows, cols] * v)
                target(lo, n, cols, jnp.where(mask_ref[rows, cols] == 1, 0.0, new))

    def fill_loads():
        n = 32
        for lo in range(0, ROWS, n):
            rows = pl.ds(lo, n)
            tap = tap_ref[rows, :]
            for step in range(STEPS):
                value = jnp.zeros(tap.shape, F32)
                for which in range(NW):
                    value = jnp.where(tap == which, wave_ref[step, which], value)
                load_ref[step, rows, :] = value

    for one in loads[:4]:
        one.wait()
    for lo in range(0, ROWS, 32):
        fill_products(0, lo, 32)
    pl.semaphore_wait(barrier, (1 + one_if(has_up) + one_if(has_down)) * (1 + one_if(has_left) + one_if(has_right)) - 1)
    send(0)

    @pl.when(has_down)
    def _():
        edge.start()

    for one in loads[4:]:
        one.wait()
    build_table(k_ref, 0, pad_ref, base_ref, table_ref)
    build_table(k_ref, 1, pad_ref, base_ref, table_ref)
    fill_loads()

    @pl.when(has_down)
    def _():
        edge.wait_send()

    @pl.when(has_up)
    def _():
        edge.wait_recv()

    for step in range(STEPS):
        receive(step)
        if step == 0:
            curl_ref[...] = froml_ref[0, TOP : TOP + ROWS, :]
        drive(step)
        convolve(0)
        convolve(1)
        advance(step)
        if step + 1 < STEPS:
            def keep(lo, n, cols, value, step=step):
                frame_ref[step + 1, 0, pl.ds(TOP + lo, n), cols] = value

            update(step, keep)
            for lo in range(0, ROWS, 32):
                fill_products(step + 1, lo, 32)
            send(step + 1)
        else:
            def keep_last(lo, n, cols, value):
                vout_ref[pl.ds(lo, n), cols] = value

            cout_ref[0] = cur0_ref[8 : 8 + ROWS, :]
            cout_ref[1] = cur1_ref[...]
            update(step, keep_last)
    for step in range(STEPS):
        drain(step)


def local(voltage, currents, resistance, inverse_cap, shunt_conductance, tap_index, pad_mask, waveforms, k_window):
    anywhere = pl.BlockSpec(memory_space=pltpu.HBM)
    vmem = pl.BlockSpec(memory_space=pltpu.VMEM)
    block = (ROWS, COLS)
    scratch = [
        pltpu.VMEM((2, *block), F32),
        pltpu.VMEM(block, F32),
        pltpu.VMEM(block, F32),
        pltpu.VMEM(block, jnp.int32),
        pltpu.VMEM(block, jnp.int32),
        pltpu.VMEM((STEPS, 3, EXT, COLS), F32),
        pltpu.VMEM((ROWS + 8, COLS), F32),
        pltpu.VMEM(block, F32),
        pltpu.VMEM((ROWS, LANES), F32),
        pltpu.VMEM((STEPS, ROWS, LANES), F32),
        pltpu.VMEM((STEPS, ROWS, LANES), F32),
        pltpu.VMEM((STEPS, EXT, LANES), F32),
        pltpu.VMEM((STEPS, EXT, LANES), F32),
        pltpu.VMEM((9, DEEP, LANES), F32),
        pltpu.VMEM((160, DEPTH), BF16),
        pltpu.VMEM((2, DEPTH, 2 * LANES), BF16),
        pltpu.VMEM((48, LANES), F32),
        pltpu.VMEM((40, LANES), F32),
        pltpu.VMEM((STEPS, *block), F32),
        pltpu.VMEM((2, ROWS + 40, LANES), F32),
        pltpu.VMEM((2, ROWS, LANES), F32),
        pltpu.VMEM((ROWS, LANES), F32),
        pltpu.SMEM((STEPS, NW), F32),
        pltpu.VMEM((SPAN, 2, SPAN), BF16),
        pltpu.SemaphoreType.DMA((10,)),
        pltpu.SemaphoreType.DMA((STEPS, 8)),
        pltpu.SemaphoreType.DMA((STEPS, 8)),
        pltpu.SemaphoreType.DMA((2,)),
    ]
    call = pl.pallas_call(
        kernel,
        out_shape=(jax.ShapeDtypeStruct(block, F32), jax.ShapeDtypeStruct((2, *block), F32)),
        in_specs=[anywhere] * 9,
        out_specs=(vmem, vmem),
        scratch_shapes=scratch,
        compiler_params=pltpu.CompilerParams(
            collective_id=0, has_side_effects=True, vmem_limit_bytes=40 * 1024 * 1024
        ),
    )
    held = [waveforms, jnp.transpose(k_window, (1, 0, 2)), voltage, currents, resistance, inverse_cap]
    held += [shunt_conductance, tap_index, pad_mask]
    held = [pltpu.with_memory_space_constraint(one, pltpu.HBM) for one in held]
    return call(*held)


def solution(mesh):
    placed = (
        P("row", "col"),
        P(None, "row", "col"),
        P(None, "row", "col"),
        P("row", "col"),
        P("row", "col"),
        P("row", "col"),
        P("row", "col"),
        P(),
        P(),
    )
    return jax.shard_map(
        local,
        mesh=mesh,
        in_specs=placed,
        out_specs=(P("row", "col"), P(None, "row", "col")),
        check_vma=False,
    )
```

time: 274 us -> 20.9 us (0.08)
  the two profiles are of different devices: /device:TPU:20 before, /device:TPU:97 now
where the time goes in v1:
time: 20.9 us; the launch traced here: 20.6 us
  Pallas kernels  18.6 us (89%)
  local copies, waits for them, and re-layouts  1.36 us (7%)
  between operations  0.64 us (3%)
    pallas_call x1, Pallas kernels, local(): return call(*held)  18.6 us
    unnamed x2, local copies, waits for them, and re-layouts  1.36 us

profile of v1, /device:TPU:97, one launch (start us, length us, event | category | flops | bytes accessed | tf_op | source)
XLA Modules:
  0.0 20.6 jit_solution(17894528303997745642)
XLA Ops:
  0.6 18.6 %shard_map.104 = (f32[128,256]{1,0:T(8,128)S(1)}, f32[2,128,256]{2,1,0:T(8,128)S(1)}) custom-call(f32[2,8]{1,0:T(2,128)} %wave_hbm.1, bf16[33,2,33]{2,1,0:T(2,128)(2,1)} %bitcast.1, f32[128,256]{1,0:T(8,128)} %v_hbm.1, f32[2,128,256]{2,1,0:T(8,128)} %c_hbm.1, f32[2,128,256]{2,1,0:T(8,128)} %r_hbm.1, f32[128,256]{1,0:T(8,128)} %cap_hbm.1, ...), custom_call_target="tpu_custom_call" | custom-call | tf_op jit(solution)/shard_map/pallas_call | solution.py:407
  19.2 0.7 %copy.13 = f32[128,256]{1,0:T(8,128)} copy(f32[128,256]{1,0:T(8,128)S(1)} %get-tuple-element.4) | data formatting | bytes 262144
  19.9 0.7 %copy.14 = f32[2,128,256]{2,1,0:T(8,128)} copy(f32[2,128,256]{2,1,0:T(8,128)S(1)} %get-tuple-element.5) | data formatting | bytes 524288

commit v2 on v0

v2 whole, which is shorter than its diff:
```python
import functools

import jax
import jax.numpy as jnp
from jax import lax
from jax.experimental import pallas as pl
from jax.experimental.pallas import tpu as pltpu
from jax.sharding import PartitionSpec as P

HALF = 16
SPAN = 2 * HALF + 1
STEPS = 2
NW = 8
ROWS = 128
COLS = 256
LANES = 128
TOP = 48
EXT = ROWS + 2 * TOP
SKIP = 8
DEEP = 232
WIDE = 34
NEAR = 18
FLOW = 200
FROM = 24
GROUP = 4
TAPS = SPAN + GROUP - 1
DEPTH = TAPS * LANES
MESH = pl.DeviceIdType.MESH
F32 = jnp.float32
BF16 = jnp.bfloat16
DIRECTIONS = ((-1, 0), (1, 0), (0, -1), (0, 1), (-1, -1), (-1, 1), (1, -1), (1, 1))


def lane_of(shape):
    return lax.broadcasted_iota(jnp.int32, shape, len(shape) - 1)


def roll(value, amount):
    return pltpu.roll(value, amount % LANES, 1)


def one_if(flag):
    return jnp.where(flag, 1, 0)


def build_table(k_ref, comp, pad_ref, base_ref, table_ref):
    pad_ref[...] = jnp.zeros_like(pad_ref)
    pad_ref[8 : 8 + SPAN, 0:SPAN] = k_ref[:, comp, :].astype(F32)
    tap = lax.broadcasted_iota(jnp.int32, (LANES, LANES), 0)
    lane = lax.broadcasted_iota(jnp.int32, (LANES, LANES), 1)
    near = jnp.where(((HALF - tap) & 127) == lane, 1.0, 0.0).astype(BF16)
    far = jnp.where(((HALF + 64 - tap) & 127) == lane, 1.0, 0.0).astype(BF16)
    near = jnp.where(tap < SPAN, near, jnp.zeros_like(near))
    far = jnp.where(tap < SPAN, far, jnp.zeros_like(far))
    here = pad_ref[8:48, :].astype(BF16)
    above = pad_ref[7:47, :].astype(BF16)
    base_ref[...] = jnp.dot(here, near, preferred_element_type=F32) + jnp.dot(above, far, preferred_element_type=F32)
    inside = ((tap - (lane & 63) + HALF) & 127) < SPAN

    def one(index, carry):
        row = jnp.broadcast_to(base_ref[pl.ds(index, 1), :], (LANES, LANES))
        turned = pltpu.roll(row, 0, 1, stride=1, stride_axis=0)
        block = jnp.where(inside, turned, 0.0).astype(BF16)
        table_ref[comp, pl.ds(pl.multiple_of(index * LANES, LANES), LANES), 0:LANES] = block
        table_ref[comp, pl.ds(pl.multiple_of((index + 2) * LANES, LANES), LANES), LANES:] = block
        return carry

    lax.fori_loop(0, SPAN + 1, one, 0)
    blank = jnp.zeros((2 * LANES, LANES), BF16)
    table_ref[comp, (SPAN + 1) * LANES :, 0:LANES] = blank
    table_ref[comp, 0 : 2 * LANES, LANES:] = blank


SLOTS = (("vh", WIDE), ("vl", WIDE), ("w0", WIDE), ("w1", WIDE), ("c0", NEAR), ("c1", NEAR), ("r0", NEAR), ("r1", NEAR), ("b", NEAR), ("q", NEAR))
ROW_BASE = {name: sum(width for _, width in SLOTS[:i]) for i, (name, _) in enumerate(SLOTS)}
WIDTH = dict(SLOTS)
LANE_TILES = (("vh", "vl", "w0", "q"), ("w1", "c0", "c1", "r0", "r1", "b"))


def lane_slots(names):
    base = 0
    for name in names:
        yield name, base
        base += WIDTH[name]


def kernel(
    wave_hbm, k_hbm, v_hbm, c_hbm, r_hbm, cap_hbm, shunt_hbm, tap_hbm, mask_hbm,
    vout_ref, cout_ref,
    cap_ref, shunt_ref, tap_ref, mask_ref,
    v_ref, w_ref, c_ref, r_ref, b_ref, q_ref,
    stage_ref, sendv_ref, sends_ref, fromv_ref, froms_ref,
    drive_ref, lhs_ref, table_ref, pad_ref, base_ref, load_ref, flow_ref,
    wave_ref, k_ref, load_sem, send_sem, recv_sem,
):
    my_row, my_col = lax.axis_index("row"), lax.axis_index("col")
    n_row, n_col = lax.axis_size("row"), lax.axis_size("col")

    def exists(dr, dc):
        row, col = my_row + dr, my_col + dc
        ok = None
        for spot, count, delta in ((row, n_row, dr), (col, n_col, dc)):
            if delta:
                here = (spot >= 0) & (spot < count)
                ok = here if ok is None else ok & here
        return ok

    own = pl.ds(TOP, ROWS)
    pairs = [(k_hbm, k_ref), (wave_hbm, wave_ref)]
    pairs += [(cap_hbm, cap_ref), (shunt_hbm, shunt_ref), (tap_hbm, tap_ref), (mask_hbm, mask_ref)]
    for p in range(2):
        cols = pl.ds(p * LANES, LANES)
        pairs.append((v_hbm.at[:, cols], v_ref.at[p + 1, own, :]))
        for comp in range(2):
            pairs.append((c_hbm.at[comp, :, cols], c_ref.at[comp, p + 1, own, :]))
            pairs.append((r_hbm.at[comp, :, cols], r_ref.at[comp, p + 1, own, :]))
    loads = [pltpu.make_async_copy(src, dst, load_sem.at[i]) for i, (src, dst) in enumerate(pairs)]
    for one in loads:
        one.start()
    barrier = pltpu.get_barrier_semaphore()
    for dr, dc in DIRECTIONS:
        @pl.when(exists(dr, dc))
        def _(dr=dr, dc=dc):
            pl.semaphore_signal(barrier, inc=1, device_id=(my_row + dr, my_col + dc), device_id_type=MESH)

    has_up, has_down, has_left, has_right = (exists(*d) for d in DIRECTIONS[:4])

    for side, missing in enumerate((has_up, has_down)):
        @pl.when(jnp.logical_not(missing))
        def _(side=side):
            fromv_ref[side] = jnp.zeros(fromv_ref.shape[1:], BF16)
            rows = pl.ds(0, TOP) if side == 0 else pl.ds(TOP + ROWS, TOP)
            for other in range(2):
                froms_ref[other, rows, :] = jnp.zeros((TOP, COLS), BF16)

    for side, missing in enumerate((has_left, has_right)):
        @pl.when(jnp.logical_not(missing))
        def _(side=side):
            froms_ref[side] = jnp.zeros(froms_ref.shape[1:], BF16)

    def message(which):
        dr, dc = DIRECTIONS[which]
        low, mid, high = pl.ds(0, TOP), pl.ds(TOP, ROWS), pl.ds(TOP + ROWS, TOP)
        first, last = pl.ds(0, TOP), pl.ds(ROWS - TOP, TOP)
        if dc == 0:
            side = 0 if dr > 0 else 1
            source, target = sendv_ref.at[1 - side], fromv_ref.at[side]
        else:
            side = 0 if dc > 0 else 1
            out, land = sends_ref.at[1 - side], froms_ref.at[side]
            source = out if dr == 0 else out.at[first if dr < 0 else last, :]
            target = land.at[mid if dr == 0 else (high if dr < 0 else low), :]
        return pltpu.make_async_remote_copy(
            src_ref=source,
            dst_ref=target,
            send_sem=send_sem.at[which],
            recv_sem=recv_sem.at[which],
            device_id=(my_row + dr, my_col + dc),
            device_id_type=MESH,
        )

    def prepare():
        n = 32
        for lo in range(0, ROWS, n):
            rows, at = pl.ds(lo, n), pl.ds(TOP + lo, n)
            for p in range(2):
                cols = slice(p * LANES, (p + 1) * LANES)
                tap = tap_ref[rows, cols]
                for step in range(STEPS):
                    value = jnp.zeros(tap.shape, F32)
                    for which in range(NW):
                        value = jnp.where(tap == which, wave_ref[step, which], value)
                    load_ref[step, rows, cols] = value
                v = v_ref[p + 1, at, :]
                cap = cap_ref[rows, cols]
                held = mask_ref[rows, cols] == 1
                b = jnp.where(held, 0.0, cap)
                q = jnp.where(held, 0.0, cap * (load_ref[0, rows, cols] - shunt_ref[rows, cols] * v))
                b_ref[p + 1, at, :] = b
                q_ref[p + 1, at, :] = q
                part = {"b": b, "q": q}
                for comp in range(2):
                    c, r = c_ref[comp, p + 1, at, :], r_ref[comp, p + 1, at, :]
                    w = r * c
                    w_ref[comp, p + 1, at, :] = w
                    part["c%d" % comp], part["r%d" % comp], part["w%d" % comp] = c, r, w
                part["vh"] = v.astype(BF16).astype(F32)
                part["vl"] = v - part["vh"]
                lane = lane_of((n, LANES))
                for tile, names in enumerate(LANE_TILES):
                    mixed = None
                    for name, base in reversed(list(lane_slots(names))):
                        turned = roll(part[name], base if p == 0 else base + WIDTH[name])
                        mixed = turned if mixed is None else jnp.where(lane < base + WIDTH[name], turned, mixed)
                    sends_ref[p, rows, tile * LANES : (tile + 1) * LANES] = mixed.astype(BF16)

    def stack():
        for p in range(2):
            cols = slice(p * LANES, (p + 1) * LANES)
            for side in range(2):
                for name, width in SLOTS:
                    at = pl.ds(TOP if side == 0 else TOP + ROWS - width, width)
                    if name[0] == "v":
                        v = v_ref[p + 1, at, :]
                        value = v.astype(BF16).astype(F32)
                        value = value if name == "vh" else v - value
                    elif name in ("b", "q"):
                        value = (b_ref if name == "b" else q_ref)[p + 1, at, :]
                    else:
                        ref = {"w": w_ref, "c": c_ref, "r": r_ref}[name[0]]
                        value = ref[int(name[1]), p + 1, at, :]
                    stage_ref[side, pl.ds(ROW_BASE[name], width), cols] = value
        for side in range(2):
            for lo in range(0, 256, 64):
                sendv_ref[side, pl.ds(lo, 64), :] = stage_ref[side, pl.ds(lo, 64), :].astype(BF16)

    def put(name, tile, at, value):
        if name in ("b", "q"):
            (b_ref if name == "b" else q_ref)[tile, at, :] = value
        else:
            ref = {"w": w_ref, "c": c_ref, "r": r_ref}[name[0]]
            ref[int(name[1]), tile, at, :] = value

    def unpack_sides():
        n = 32
        for side in range(2):
            tile = 3 * side
            for lo in range(0, EXT, n):
                at = pl.ds(lo, n)
                got = {}
                for half, names in enumerate(LANE_TILES):
                    value = froms_ref[side, at, half * LANES : (half + 1) * LANES].astype(F32)
                    for name, base in lane_slots(names):
                        got[name] = roll(value, -(base + WIDTH[name]) if side == 0 else -base)
                v_ref[tile, at, :] = got["vh"] + got["vl"]
                for name in got:
                    if name[0] != "v":
                        put(name, tile, at, got[name])

    def unpack_ends():
        for side in range(2):
            for lo in range(0, 256, 64):
                stage_ref[side, pl.ds(lo, 64), :] = fromv_ref[side, pl.ds(lo, 64), :].astype(F32)
            for p in range(2):
                cols = slice(p * LANES, (p + 1) * LANES)
                for name, width in SLOTS:
                    at = pl.ds(TOP - width if side == 0 else TOP + ROWS, width)
                    value = stage_ref[side, pl.ds(ROW_BASE[name], width), cols]
                    if name == "vh":
                        v_ref[p + 1, at, :] = value + stage_ref[side, pl.ds(ROW_BASE["vl"], width), cols]
                    elif name != "vl":
                        put(name, p + 1, at, value)

    def drive(step):
        reach = WIDE if step == 0 else NEAR - 1
        lo = jnp.where(has_up, TOP - reach, TOP)
        hi = jnp.where(has_down, TOP + ROWS + reach - 1, TOP + ROWS)
        start, stop, n = (SKIP, EXT - SKIP, 16) if step == 0 else (FROM, EXT - FROM, 16)
        for base in range(start, stop, n):
            at, nxt, to = pl.ds(base, n), pl.ds(base + 1, n), pl.ds(base - SKIP, n)
            row = lax.broadcasted_iota(jnp.int32, (n, LANES), 0) + base
            lane = lane_of((n, LANES))
            inside = (row >= lo) & (row < hi)
            held = [inside & has_left, inside, inside, inside & has_right]
            v = [v_ref[k, at, :] for k in range(4)]
            for comp in range(2):
                out = []
                for k in range(4):
                    if step == 0:
                        w = w_ref[comp, k, at, :]
                    else:
                        w = r_ref[comp, k, at, :] * c_ref[comp, k, at, :]
                    if comp == 0:
                        beside = v_ref[k, nxt, :]
                    else:
                        beside = roll(jnp.where(lane == 0, v[min(k + 1, 3)], v[k]), LANES - 1)
                    out.append(jnp.where(held[k], v[k] - beside - w, 0.0))
                tl, ta, tb, tr = out
                slot = 6 * comp
                if step == 0 or comp == 1:
                    drive_ref[slot, to, :] = roll(jnp.where(lane < 64, ta, tl), 64)
                drive_ref[slot + 1, to, :] = jnp.where(lane < 96, ta, tl)
                drive_ref[slot + 2, to, :] = roll(jnp.where(lane < 32, tb, ta), 64)
                drive_ref[slot + 3, to, :] = jnp.where(lane < 96, tb, ta)
                drive_ref[slot + 4, to, :] = roll(jnp.where(lane < 32, tr, tb), 64)
                if step == 0:
                    drive_ref[slot + 5, to, :] = jnp.where(lane < 96, tr, tb)

    def convolve(step, comp):
        if step == 0:
            blocks, start, n, to = (-1, 0, 1, 2, 3, 4), 4, 48, 4
        elif comp == 0:
            blocks, start, n, to = (0, 1, 2, 3), 20, 40, 20
        else:
            blocks, start, n, to = (-1, 0, 1, 2, 3), 24, 32, 24
        total = n * len(blocks)
        for tap in range(TAPS):
            pieces = [drive_ref[6 * comp + 1 + k, pl.ds(start + tap, n, stride=GROUP), :] for k in blocks]
            lhs_ref[0:total, tap * LANES : (tap + 1) * LANES] = jnp.concatenate(pieces, axis=0).astype(BF16)
        product = jnp.dot(lhs_ref[0:total, :], table_ref[comp], preferred_element_type=F32)
        low = lane_of((n, LANES)) < 64
        for t in range(GROUP):
            half = product[:, (t // 2) * LANES : (t // 2 + 1) * LANES]
            part = {k: half[i * n : (i + 1) * n] for i, k in enumerate(blocks)}
            for tile, (even, odd) in enumerate(((None, -1), (0, 1), (2, 3), (4, None))):
                if even not in part and odd not in part:
                    continue
                if even is None:
                    value = roll(part[odd], 64) if t % 2 == 0 else part[odd]
                elif odd is None:
                    value = part[even] if t % 2 == 0 else roll(part[even], 64)
                elif t % 2 == 0:
                    value = jnp.where(low, part[even], roll(part[odd], 64))
                else:
                    value = jnp.where(low, roll(part[even], 64), part[odd])
                flow_ref[comp, tile, pl.ds(to + t, n, stride=GROUP), :] = value

    def advance_frame():
        n = 16
        lo = jnp.where(has_up, 0, TOP)
        hi = jnp.where(has_down, EXT, TOP + ROWS)
        for base in range(FROM, EXT - FROM, n):
            at, flow = pl.ds(base, n), pl.ds(base - FROM, n)
            row = lax.broadcasted_iota(jnp.int32, (n, LANES), 0) + base
            inside = (row >= lo) & (row < hi)
            held = [inside & has_left, inside, inside, inside & has_right]
            for comp in range(2):
                for k in range(4):
                    value = c_ref[comp, k, at, :] + flow_ref[comp, k, flow, :]
                    c_ref[comp, k, at, :] = jnp.where(held[k], value, 0.0)

    def divergence(base, n, k):
        at = pl.ds(base, n)
        lane = lane_of((n, LANES))
        c1 = c_ref[1, k, at, :]
        before_x = c_ref[0, k, pl.ds(base - 1, n), :]
        before_y = roll(jnp.where(lane == LANES - 1, c_ref[1, max(k - 1, 0), at, :], c1), 1)
        return c_ref[0, k, at, :] - before_x + c1 - before_y

    def update_frame():
        n = 16
        for base in range(FROM, EXT - FROM, n):
            at = pl.ds(base, n)
            for k in range(4):
                b = b_ref[k, at, :]
                value = v_ref[k, at, :] + q_ref[k, at, :] - b * divergence(base, n, k)
                v_ref[k, at, :] = jnp.where(b == 0.0, 0.0, value)

    def finish():
        n = 32
        for k in range(1, 3):
            at = pl.ds(TOP - 8, 8)
            head = c_ref[0, k, at, :] + flow_ref[0, k, pl.ds(TOP - 8 - FROM, 8), :]
            c_ref[0, k, at, :] = jnp.where(has_up, head, 0.0)
        for lo in range(0, ROWS, n):
            at, flow = pl.ds(TOP + lo, n), pl.ds(TOP + lo - FROM, n)
            left = c_ref[1, 0, at, :] + flow_ref[1, 0, flow, :]
            c_ref[1, 0, at, :] = jnp.where(has_left, left, 0.0)
            for k in range(1, 3):
                cols = slice((k - 1) * LANES, k * LANES)
                for comp in range(2):
                    value = c_ref[comp, k, at, :] + flow_ref[comp, k, flow, :]
                    c_ref[comp, k, at, :] = value
                    cout_ref[comp, pl.ds(lo, n), cols] = value
        for lo in range(0, ROWS, n):
            at, rows = pl.ds(TOP + lo, n), pl.ds(lo, n)
            for k in range(1, 3):
                cols = slice((k - 1) * LANES, k * LANES)
                v = v_ref[k, at, :]
                change = load_ref[1, rows, cols] - divergence(TOP + lo, n, k) - shunt_ref[rows, cols] * v
                vout_ref[rows, cols] = jnp.where(mask_ref[rows, cols] == 1, 0.0, v + cap_ref[rows, cols] * change)

    for one in loads:
        one.wait()
    prepare()
    stack()
    pl.semaphore_wait(barrier, (1 + one_if(has_up) + one_if(has_down)) * (1 + one_if(has_left) + one_if(has_right)) - 1)
    for which, (dr, dc) in enumerate(DIRECTIONS):
        @pl.when(exists(dr, dc))
        def _(which=which):
            message(which).start()
    build_table(k_ref, 0, pad_ref, base_ref, table_ref)
    build_table(k_ref, 1, pad_ref, base_ref, table_ref)
    for which, (dr, dc) in enumerate(DIRECTIONS):
        @pl.when(exists(-dr, -dc))
        def _(which=which):
            message(which).wait_recv()
    unpack_sides()
    unpack_ends()
    drive(0)
    convolve(0, 0)
    convolve(0, 1)
    advance_frame()
    update_frame()
    drive(1)
    convolve(1, 0)
    convolve(1, 1)
    finish()
    for which, (dr, dc) in enumerate(DIRECTIONS):
        @pl.when(exists(dr, dc))
        def _(which=which):
            message(which).wait_send()


def local(voltage, currents, resistance, inverse_cap, shunt_conductance, tap_index, pad_mask, waveforms, k_window):
    hbm = pl.BlockSpec(memory_space=pltpu.HBM)
    vmem = pl.BlockSpec(memory_space=pltpu.VMEM)
    block = (ROWS, COLS)
    frame = (4, EXT, LANES)
    scratch = [
        pltpu.VMEM(block, F32),
        pltpu.VMEM(block, F32),
        pltpu.VMEM(block, jnp.int32),
        pltpu.VMEM(block, jnp.int32),
        pltpu.VMEM(frame, F32),
        pltpu.VMEM((2, *frame), F32),
        pltpu.VMEM((2, *frame), F32),
        pltpu.VMEM((2, *frame), F32),
        pltpu.VMEM(frame, F32),
        pltpu.VMEM(frame, F32),
        pltpu.VMEM((2, 256, COLS), F32),
        pltpu.VMEM((2, 256, COLS), BF16),
        pltpu.VMEM((2, ROWS, COLS), BF16),
        pltpu.VMEM((2, 256, COLS), BF16),
        pltpu.VMEM((2, EXT, COLS), BF16),
        pltpu.VMEM((12, DEEP, LANES), F32),
        pltpu.VMEM((288, DEPTH), BF16),
        pltpu.VMEM((2, DEPTH, 2 * LANES), BF16),
        pltpu.VMEM((48, LANES), F32),
        pltpu.VMEM((40, LANES), F32),
        pltpu.VMEM((STEPS, *block), F32),
        pltpu.VMEM((2, 4, FLOW, LANES), F32),
        pltpu.SMEM((STEPS, NW), F32),
        pltpu.VMEM((SPAN, 2, SPAN), BF16),
        pltpu.SemaphoreType.DMA((16,)),
        pltpu.SemaphoreType.DMA((8,)),
        pltpu.SemaphoreType.DMA((8,)),
    ]
    call = pl.pallas_call(
        kernel,
        out_shape=(jax.ShapeDtypeStruct(block, F32), jax.ShapeDtypeStruct((2, *block), F32)),
        in_specs=[hbm] * 9,
        out_specs=(vmem, vmem),
        scratch_shapes=scratch,
        compiler_params=pltpu.CompilerParams(
            collective_id=0, has_side_effects=True, vmem_limit_bytes=40 * 1024 * 1024
        ),
    )
    held = [waveforms, jnp.transpose(k_window, (1, 0, 2)), voltage, currents, resistance, inverse_cap]
    held += [shunt_conductance, tap_index, pad_mask]
    held = [pltpu.with_memory_space_constraint(one, pltpu.HBM) for one in held]
    return call(*held)


def solution(mesh):
    placed = (
        P("row", "col"),
        P(None, "row", "col"),
        P(None, "row", "col"),
        P("row", "col"),
        P("row", "col"),
        P("row", "col"),
        P("row", "col"),
        P(),
        P(),
    )
    return jax.shard_map(
        local,
        mesh=mesh,
        in_specs=placed,
        out_specs=(P("row", "col"), P(None, "row", "col")),
        check_vma=False,
    )
```

time: 274 us -> 17.8 us (0.06)
  the two profiles are of different devices: /device:TPU:20 before, /device:TPU:97 now
where the time goes in v2:
time: 17.8 us; the launch traced here: 17.6 us
  Pallas kernels  15.6 us (88%)
  local copies, waits for them, and re-layouts  1.36 us (8%)
  between operations  0.64 us (4%)
    pallas_call x1, Pallas kernels, local(): return call(*held)  15.6 us
    unnamed x2, local copies, waits for them, and re-layouts  1.36 us

profile of v2, /device:TPU:97, one launch (start us, length us, event | category | flops | bytes accessed | tf_op | source)
XLA Modules:
  0.0 17.6 jit_solution(17886349282455458743)
XLA Ops:
  0.6 15.6 %shard_map.104 = (f32[128,256]{1,0:T(8,128)S(1)}, f32[2,128,256]{2,1,0:T(8,128)S(1)}) custom-call(f32[2,8]{1,0:T(2,128)} %wave_hbm.1, bf16[33,2,33]{2,1,0:T(2,128)(2,1)} %bitcast.1, f32[128,256]{1,0:T(8,128)} %v_hbm.1, f32[2,128,256]{2,1,0:T(8,128)} %c_hbm.1, f32[2,128,256]{2,1,0:T(8,128)} %r_hbm.1, f32[128,256]{1,0:T(8,128)} %cap_hbm.1, ...), custom_call_target="tpu_custom_call" | custom-call | tf_op jit(solution)/shard_map/pallas_call | solution.py:452
  16.3 0.7 %copy.13 = f32[128,256]{1,0:T(8,128)} copy(f32[128,256]{1,0:T(8,128)S(1)} %get-tuple-element.4) | data formatting | bytes 262144
  16.9 0.7 %copy.14 = f32[2,128,256]{2,1,0:T(8,128)} copy(f32[2,128,256]{2,1,0:T(8,128)S(1)} %get-tuple-element.5) | data formatting | bytes 524288

commit v3 on v2

--- a/solution.py
+++ b/solution.py
@@ -17,14 +17,17 @@
 TOP = 48
 EXT = ROWS + 2 * TOP
 SKIP = 8
-DEEP = 232
+PITCH = 33
 WIDE = 34
 NEAR = 18
-FLOW = 200
+FLOW = 27
 FROM = 24
-GROUP = 4
+GROUP = 8
+STRIP = LANES // 4
 TAPS = SPAN + GROUP - 1
-DEPTH = TAPS * LANES
+CHUNKS = TAPS // 2
+DEPTH = CHUNKS * LANES
+BLOCKS = CHUNKS - 2
 MESH = pl.DeviceIdType.MESH
 F32 = jnp.float32
 BF16 = jnp.bfloat16
@@ -43,32 +46,45 @@
     return jnp.where(flag, 1, 0)
 
 
-def build_table(k_ref, comp, pad_ref, base_ref, table_ref):
-    pad_ref[...] = jnp.zeros_like(pad_ref)
-    pad_ref[8 : 8 + SPAN, 0:SPAN] = k_ref[:, comp, :].astype(F32)
+def build_table(k_ref, pad_ref, base_ref, table_ref):
     tap = lax.broadcasted_iota(jnp.int32, (LANES, LANES), 0)
     lane = lax.broadcasted_iota(jnp.int32, (LANES, LANES), 1)
-    near = jnp.where(((HALF - tap) & 127) == lane, 1.0, 0.0).astype(BF16)
-    far = jnp.where(((HALF + 64 - tap) & 127) == lane, 1.0, 0.0).astype(BF16)
-    near = jnp.where(tap < SPAN, near, jnp.zeros_like(near))
-    far = jnp.where(tap < SPAN, far, jnp.zeros_like(far))
-    here = pad_ref[8:48, :].astype(BF16)
-    above = pad_ref[7:47, :].astype(BF16)
-    base_ref[...] = jnp.dot(here, near, preferred_element_type=F32) + jnp.dot(above, far, preferred_element_type=F32)
-    inside = ((tap - (lane & 63) + HALF) & 127) < SPAN
+    for comp in range(2):
+        pad_ref[comp] = jnp.zeros(pad_ref.shape[1:], F32)
+        pad_ref[comp, 8 : 8 + SPAN, 0:SPAN] = k_ref[:, comp, :].astype(F32)
+        for kind in range(2):
+            total = None
+            for t in range(4):
+                hit = (((STRIP * t + HALF - tap) & 127) == lane) & (tap >= kind) & (tap < SPAN - 1 + kind)
+                rows = pad_ref[comp, 8 - t : 48 - t, :].astype(BF16)
+                part = jnp.dot(rows, jnp.where(hit, 1.0, 0.0).astype(BF16), preferred_element_type=F32)
+                total = part if total is None else total + part
+            base_ref[comp, kind] = total
+    within = lax.broadcasted_iota(jnp.int32, (64, LANES), 0)
+    strip = lax.broadcasted_iota(jnp.int32, (64, LANES), 1) & (STRIP - 1)
+    inside = ((within - strip + HALF) & 63) < SPAN
+
+    def turned(row, count, shift):
+        return pltpu.roll(jnp.broadcast_to(row, (count, LANES)), shift, 1, stride=1, stride_axis=0)
 
     def one(index, carry):
-        row = jnp.broadcast_to(base_ref[pl.ds(index, 1), :], (LANES, LANES))
-        turned = pltpu.roll(row, 0, 1, stride=1, stride_axis=0)
-        block = jnp.where(inside, turned, 0.0).astype(BF16)
-        table_ref[comp, pl.ds(pl.multiple_of(index * LANES, LANES), LANES), 0:LANES] = block
-        table_ref[comp, pl.ds(pl.multiple_of((index + 2) * LANES, LANES), LANES), LANES:] = block
+        for comp in range(2):
+            halves = []
+            for odd in range(2):
+                near = base_ref[comp, 0, pl.ds(2 * index + odd, 1), :]
+                far = base_ref[comp, 1, pl.ds(2 * index + odd, 1), :]
+                whole = [turned(near, 16, 0), turned(far, 32, 16), turned(near, 16, LANES - 16)]
+                halves.append(jnp.where(inside, jnp.concatenate(whole, axis=0), 0.0))
+            block = jnp.concatenate(halves, axis=0).astype(BF16)
+            table_ref[comp, pl.ds(pl.multiple_of(index * LANES, LANES), LANES), 0:LANES] = block
+            table_ref[comp, pl.ds(pl.multiple_of((index + 2) * LANES, LANES), LANES), LANES:] = block
         return carry
 
-    lax.fori_loop(0, SPAN + 1, one, 0)
+    lax.fori_loop(0, BLOCKS, one, 0, unroll=2)
     blank = jnp.zeros((2 * LANES, LANES), BF16)
-    table_ref[comp, (SPAN + 1) * LANES :, 0:LANES] = blank
-    table_ref[comp, 0 : 2 * LANES, LANES:] = blank
+    for comp in range(2):
+        table_ref[comp, BLOCKS * LANES :, 0:LANES] = blank
+        table_ref[comp, 0 : 2 * LANES, LANES:] = blank
 
 
 SLOTS = (("vh", WIDE), ("vl", WIDE), ("w0", WIDE), ("w1", WIDE), ("c0", NEAR), ("c1", NEAR), ("r0", NEAR), ("r1", NEAR), ("b", NEAR), ("q", NEAR))
@@ -90,7 +106,7 @@
     cap_ref, shunt_ref, tap_ref, mask_ref,
     v_ref, w_ref, c_ref, r_ref, b_ref, q_ref,
     stage_ref, sendv_ref, sends_ref, fromv_ref, froms_ref,
-    drive_ref, lhs_ref, table_ref, pad_ref, base_ref, load_ref, flow_ref,
+    drive_ref, table_ref, pad_ref, base_ref, load_ref, flow_ref,
     wave_ref, k_ref, load_sem, send_sem, recv_sem,
 ):
     my_row, my_col = lax.axis_index("row"), lax.axis_index("col")
@@ -251,19 +267,38 @@
                     elif name != "vl":
                         put(name, p + 1, at, value)
 
-    def drive(step):
+    def windows(tiles, nexts, wanted):
+        lane = lane_of(tiles[0].shape)
+        mark, low = lane & 63, lane < 64
+        pair = {}
+        for at in range(4):
+            if at > 0:
+                pair[2 * at - 2] = jnp.where(low, tiles[at], roll(nexts[at], 64))
+            if at < 3:
+                pair[2 * at - 1] = jnp.where(low, roll(tiles[at], 64), nexts[at])
+        out = {}
+        for k in wanted:
+            i = k // 2
+            if k % 2 == 0:
+                out[k] = jnp.where(mark < 48, pair[i], pair[i - 1])
+            else:
+                out[k] = jnp.where(mark < 16, pair[i + 1], pair[i])
+        return out
+
+    def drive(step, comp):
         reach = WIDE if step == 0 else NEAR - 1
         lo = jnp.where(has_up, TOP - reach, TOP)
         hi = jnp.where(has_down, TOP + ROWS + reach - 1, TOP + ROWS)
         start, stop, n = (SKIP, EXT - SKIP, 16) if step == 0 else (FROM, EXT - FROM, 16)
-        for base in range(start, stop, n):
-            at, nxt, to = pl.ds(base, n), pl.ds(base + 1, n), pl.ds(base - SKIP, n)
+        carried = {}
+        for base in reversed(range(start, stop, n)):
+            at, nxt = pl.ds(base, n), pl.ds(base + 1, n)
             row = lax.broadcasted_iota(jnp.int32, (n, LANES), 0) + base
             lane = lane_of((n, LANES))
             inside = (row >= lo) & (row < hi)
             held = [inside & has_left, inside, inside, inside & has_right]
             v = [v_ref[k, at, :] for k in range(4)]
-            for comp in range(2):
+            if True:
                 out = []
                 for k in range(4):
                     if step == 0:
@@ -275,58 +310,71 @@
                     else:
                         beside = roll(jnp.where(lane == 0, v[min(k + 1, 3)], v[k]), LANES - 1)
                     out.append(jnp.where(held[k], v[k] - beside - w, 0.0))
-                tl, ta, tb, tr = out
-                slot = 6 * comp
-                if step == 0 or comp == 1:
-                    drive_ref[slot, to, :] = roll(jnp.where(lane < 64, ta, tl), 64)
-                drive_ref[slot + 1, to, :] = jnp.where(lane < 96, ta, tl)
-                drive_ref[slot + 2, to, :] = roll(jnp.where(lane < 32, tb, ta), 64)
-                drive_ref[slot + 3, to, :] = jnp.where(lane < 96, tb, ta)
-                drive_ref[slot + 4, to, :] = roll(jnp.where(lane < 32, tr, tb), 64)
-                if step == 0:
-                    drive_ref[slot + 5, to, :] = jnp.where(lane < 96, tr, tb)
+                nexts = []
+                for k in range(4):
+                    after = carried.get((comp, k), out[k][0:8])
+                    nexts.append(pltpu.roll(jnp.concatenate([out[k], after], axis=0), n + 7, 0)[0:n])
+                    carried[comp, k] = out[k][0:8]
+                for k, value in windows(out, nexts, blocks_of(step, comp)).items():
+                    for g in range(n // 8):
+                        spot = pl.ds((base - SKIP) // 8 + g, 8, stride=PITCH)
+                        drive_ref[10 * comp + k + 1, spot, :] = value[8 * g : 8 * g + 8]
+
+    def blocks_of(step, comp):
+        if step == 0:
+            return tuple(range(-1, 9))
+        return tuple(range(0, 8)) if comp == 0 else tuple(range(-1, 8))
 
     def convolve(step, comp):
-        if step == 0:
-            blocks, start, n, to = (-1, 0, 1, 2, 3, 4), 4, 48, 4
-        elif comp == 0:
-            blocks, start, n, to = (0, 1, 2, 3), 20, 40, 20
-        else:
-            blocks, start, n, to = (-1, 0, 1, 2, 3), 24, 32, 24
-        total = n * len(blocks)
-        for tap in range(TAPS):
-            pieces = [drive_ref[6 * comp + 1 + k, pl.ds(start + tap, n, stride=GROUP), :] for k in blocks]
-            lhs_ref[0:total, tap * LANES : (tap + 1) * LANES] = jnp.concatenate(pieces, axis=0).astype(BF16)
-        product = jnp.dot(lhs_ref[0:total, :], table_ref[comp], preferred_element_type=F32)
-        low = lane_of((n, LANES)) < 64
-        for t in range(GROUP):
-            half = product[:, (t // 2) * LANES : (t // 2 + 1) * LANES]
-            part = {k: half[i * n : (i + 1) * n] for i, k in enumerate(blocks)}
-            for tile, (even, odd) in enumerate(((None, -1), (0, 1), (2, 3), (4, None))):
-                if even not in part and odd not in part:
-                    continue
-                if even is None:
-                    value = roll(part[odd], 64) if t % 2 == 0 else part[odd]
-                elif odd is None:
-                    value = part[even] if t % 2 == 0 else roll(part[even], 64)
-                elif t % 2 == 0:
-                    value = jnp.where(low, part[even], roll(part[odd], 64))
-                else:
-                    value = jnp.where(low, roll(part[even], 64), part[odd])
-                flow_ref[comp, tile, pl.ds(to + t, n, stride=GROUP), :] = value
+        blocks = blocks_of(step, comp)
+        start, n = (0, 24) if step == 0 else ((16, 24) if comp == 0 else (24, 16))
+        part = [{}, {}]
+        for odd in range(2):
+            mine = [k for k in blocks if k % 2 == odd]
+            columns = []
+            for chunk in range(CHUNKS):
+                group, phase = divmod(2 * chunk, 8)
+                at = pl.ds(phase * PITCH + start // 8 + group, n)
+                columns.append(jnp.concatenate([drive_ref[10 * comp + 1 + k, at, :] for k in mine], axis=0).astype(BF16))
+            if odd:
+                order = [(i ^ 1) * 32 for i in range(DEPTH // 32)]
+                weights = jnp.concatenate([table_ref[comp, lo : lo + 32, :] for lo in order], axis=0)
+            else:
+                weights = table_ref[comp]
+            product = jnp.dot(jnp.concatenate(columns, axis=1), weights, preferred_element_type=F32)
+            for i, k in enumerate(mine):
+                for side in range(2):
+                    part[side][k] = product[i * n : (i + 1) * n, side * LANES : (side + 1) * LANES]
+        lane = lane_of((n, LANES))
+        for side in range(2):
+            for t in range(4):
+                for tile in range(4):
+                    value = None
+                    for q in reversed(range(4)):
+                        k = 4 * (tile - 1) + q
+                        if k in part[side]:
+                            turn = (q - t) % 4
+                            piece = roll(part[side][k], STRIP * turn) if turn else part[side][k]
+                            value = piece if value is None else jnp.where(lane < STRIP * (q + 1), piece, value)
+                    if value is not None:
+                        flow_ref[comp, tile, pl.ds((4 * side + t) * FLOW + start // 8, n), :] = value
+
+    def flow(comp, tile, first, n):
+        parts = [flow_ref[comp, tile, pl.ds(first // 8 + g, 8, stride=FLOW), :] for g in range(n // 8)]
+        return jnp.concatenate(parts, axis=0) if len(parts) > 1 else parts[0]
 
     def advance_frame():
         n = 16
         lo = jnp.where(has_up, 0, TOP)
         hi = jnp.where(has_down, EXT, TOP + ROWS)
         for base in range(FROM, EXT - FROM, n):
-            at, flow = pl.ds(base, n), pl.ds(base - FROM, n)
+            at = pl.ds(base, n)
             row = lax.broadcasted_iota(jnp.int32, (n, LANES), 0) + base
             inside = (row >= lo) & (row < hi)
             held = [inside & has_left, inside, inside, inside & has_right]
             for comp in range(2):
                 for k in range(4):
-                    value = c_ref[comp, k, at, :] + flow_ref[comp, k, flow, :]
+                    value = c_ref[comp, k, at, :] + flow(comp, k, base - FROM, n)
                     c_ref[comp, k, at, :] = jnp.where(held[k], value, 0.0)
 
     def divergence(base, n, k):
@@ -350,16 +398,16 @@
         n = 32
         for k in range(1, 3):
             at = pl.ds(TOP - 8, 8)
-            head = c_ref[0, k, at, :] + flow_ref[0, k, pl.ds(TOP - 8 - FROM, 8), :]
+            head = c_ref[0, k, at, :] + flow(0, k, TOP - 8 - FROM, 8)
             c_ref[0, k, at, :] = jnp.where(has_up, head, 0.0)
         for lo in range(0, ROWS, n):
-            at, flow = pl.ds(TOP + lo, n), pl.ds(TOP + lo - FROM, n)
-            left = c_ref[1, 0, at, :] + flow_ref[1, 0, flow, :]
+            at, first = pl.ds(TOP + lo, n), TOP + lo - FROM
+            left = c_ref[1, 0, at, :] + flow(1, 0, first, n)
             c_ref[1, 0, at, :] = jnp.where(has_left, left, 0.0)
             for k in range(1, 3):
                 cols = slice((k - 1) * LANES, k * LANES)
                 for comp in range(2):
-                    value = c_ref[comp, k, at, :] + flow_ref[comp, k, flow, :]
+                    value = c_ref[comp, k, at, :] + flow(comp, k, first, n)
                     c_ref[comp, k, at, :] = value
                     cout_ref[comp, pl.ds(lo, n), cols] = value
         for lo in range(0, ROWS, n):
@@ -379,22 +427,21 @@
         @pl.when(exists(dr, dc))
         def _(which=which):
             message(which).start()
-    build_table(k_ref, 0, pad_ref, base_ref, table_ref)
-    build_table(k_ref, 1, pad_ref, base_ref, table_ref)
+    build_table(k_ref, pad_ref, base_ref, table_ref)
     for which, (dr, dc) in enumerate(DIRECTIONS):
         @pl.when(exists(-dr, -dc))
         def _(which=which):
             message(which).wait_recv()
     unpack_sides()
     unpack_ends()
-    drive(0)
-    convolve(0, 0)
-    convolve(0, 1)
+    for comp in range(2):
+        drive(0, comp)
+        convolve(0, comp)
     advance_frame()
     update_frame()
-    drive(1)
-    convolve(1, 0)
-    convolve(1, 1)
+    for comp in range(2):
+        drive(1, comp)
+        convolve(1, comp)
     finish()
     for which, (dr, dc) in enumerate(DIRECTIONS):
         @pl.when(exists(dr, dc))
@@ -423,13 +470,12 @@
         pltpu.VMEM((2, ROWS, COLS), BF16),
         pltpu.VMEM((2, 256, COLS), BF16),
         pltpu.VMEM((2, EXT, COLS), BF16),
-        pltpu.VMEM((12, DEEP, LANES), F32),
-        pltpu.VMEM((288, DEPTH), BF16),
+        pltpu.VMEM((20, 8 * PITCH, LANES), F32),
         pltpu.VMEM((2, DEPTH, 2 * LANES), BF16),
-        pltpu.VMEM((48, LANES), F32),
-        pltpu.VMEM((40, LANES), F32),
+        pltpu.VMEM((2, 48, LANES), F32),
+        pltpu.VMEM((2, 2, 40, LANES), F32),
         pltpu.VMEM((STEPS, *block), F32),
-        pltpu.VMEM((2, 4, FLOW, LANES), F32),
+        pltpu.VMEM((2, 4, 8 * FLOW, LANES), F32),
         pltpu.SMEM((STEPS, NW), F32),
         pltpu.VMEM((SPAN, 2, SPAN), BF16),
         pltpu.SemaphoreType.DMA((16,)),

time: 17.8 us -> 14.8 us (0.83)
  Pallas kernels: 15.6 us -> 12.6 us
    pallas_call x1, Pallas kernels: 15.6 us -> 12.6 us  [local(): return call(*held)]
where the time goes in v3:
time: 14.8 us; the launch traced here: 14.7 us
  Pallas kernels  12.6 us (85%)
  local copies, waits for them, and re-layouts  1.36 us (9%)
  between operations  0.64 us (4%)
    pallas_call x1, Pallas kernels, local(): return call(*held)  12.6 us
    unnamed x2, local copies, waits for them, and re-layouts  1.36 us

profile of v3, /device:TPU:97, one launch (start us, length us, event | category | flops | bytes accessed | tf_op | source)
XLA Modules:
  0.0 14.7 jit_solution(3192270065452699074)
XLA Ops:
  0.6 12.6 %shard_map.104 = (f32[128,256]{1,0:T(8,128)S(1)}, f32[2,128,256]{2,1,0:T(8,128)S(1)}) custom-call(f32[2,8]{1,0:T(2,128)} %wave_hbm.1, bf16[33,2,33]{2,1,0:T(2,128)(2,1)} %bitcast.1, f32[128,256]{1,0:T(8,128)} %v_hbm.1, f32[2,128,256]{2,1,0:T(8,128)} %c_hbm.1, f32[2,128,256]{2,1,0:T(8,128)} %r_hbm.1, f32[128,256]{1,0:T(8,128)} %cap_hbm.1, ...), custom_call_target="tpu_custom_call" | custom-call | tf_op jit(solution)/shard_map/pallas_call | solution.py:498
  13.3 0.7 %copy.13 = f32[128,256]{1,0:T(8,128)} copy(f32[128,256]{1,0:T(8,128)S(1)} %get-tuple-element.4) | data formatting | bytes 262144
  13.9 0.7 %copy.14 = f32[2,128,256]{2,1,0:T(8,128)} copy(f32[2,128,256]{2,1,0:T(8,128)S(1)} %get-tuple-element.5) | data formatting | bytes 524288

commit v4 on v3

--- a/solution.py
+++ b/solution.py
@@ -131,14 +131,14 @@
             pairs.append((c_hbm.at[comp, :, cols], c_ref.at[comp, p + 1, own, :]))
             pairs.append((r_hbm.at[comp, :, cols], r_ref.at[comp, p + 1, own, :]))
     loads = [pltpu.make_async_copy(src, dst, load_sem.at[i]) for i, (src, dst) in enumerate(pairs)]
-    for one in loads:
-        one.start()
     barrier = pltpu.get_barrier_semaphore()
     for dr, dc in DIRECTIONS:
         @pl.when(exists(dr, dc))
         def _(dr=dr, dc=dc):
             pl.semaphore_signal(barrier, inc=1, device_id=(my_row + dr, my_col + dc), device_id_type=MESH)
 
+    for one in loads:
+        one.start()
     has_up, has_down, has_left, has_right = (exists(*d) for d in DIRECTIONS[:4])
 
     for side, missing in enumerate((has_up, has_down)):
@@ -237,16 +237,18 @@
             ref = {"w": w_ref, "c": c_ref, "r": r_ref}[name[0]]
             ref[int(name[1]), tile, at, :] = value
 
-    def unpack_sides():
-        n = 32
+    def unpack_sides(first, last, n):
         for side in range(2):
             tile = 3 * side
-            for lo in range(0, EXT, n):
+            for lo in range(first, last, n):
                 at = pl.ds(lo, n)
+                near = lo + n > FROM and lo < EXT - FROM
                 got = {}
                 for half, names in enumerate(LANE_TILES):
                     value = froms_ref[side, at, half * LANES : (half + 1) * LANES].astype(F32)
                     for name, base in lane_slots(names):
+                        if WIDTH[name] == NEAR and not near:
+                            continue
                         got[name] = roll(value, -(base + WIDTH[name]) if side == 0 else -base)
                 v_ref[tile, at, :] = got["vh"] + got["vl"]
                 for name in got:
@@ -272,10 +274,11 @@
         mark, low = lane & 63, lane < 64
         pair = {}
         for at in range(4):
+            crossed = roll(jnp.where(low, nexts[at], tiles[at]), 64)
             if at > 0:
-                pair[2 * at - 2] = jnp.where(low, tiles[at], roll(nexts[at], 64))
+                pair[2 * at - 2] = jnp.where(low, tiles[at], crossed)
             if at < 3:
-                pair[2 * at - 1] = jnp.where(low, roll(tiles[at], 64), nexts[at])
+                pair[2 * at - 1] = jnp.where(low, crossed, nexts[at])
         out = {}
         for k in wanted:
             i = k // 2
@@ -285,40 +288,46 @@
                 out[k] = jnp.where(mark < 16, pair[i + 1], pair[i])
         return out
 
-    def drive(step, comp):
+    def driving(step, comp, base, n):
         reach = WIDE if step == 0 else NEAR - 1
         lo = jnp.where(has_up, TOP - reach, TOP)
         hi = jnp.where(has_down, TOP + ROWS + reach - 1, TOP + ROWS)
-        start, stop, n = (SKIP, EXT - SKIP, 16) if step == 0 else (FROM, EXT - FROM, 16)
-        carried = {}
+        at, nxt = pl.ds(base, n), pl.ds(base + 1, n)
+        row = lax.broadcasted_iota(jnp.int32, (n, LANES), 0) + base
+        lane = lane_of((n, LANES))
+        inside = (row >= lo) & (row < hi)
+        held = [inside & has_left, inside, inside, inside & has_right]
+        v = [v_ref[k, at, :] for k in range(4)]
+        out = []
+        for k in range(4):
+            if step == 0:
+                w = w_ref[comp, k, at, :]
+            else:
+                w = r_ref[comp, k, at, :] * c_ref[comp, k, at, :]
+            if comp == 0:
+                beside = v_ref[k, nxt, :]
+            else:
+                beside = roll(jnp.where(lane == 0, v[min(k + 1, 3)], v[k]), LANES - 1)
+            out.append(jnp.where(held[k], v[k] - beside - w, 0.0))
+        return out
+
+    def drive(step, comp, start, stop):
+        n = 16
+        carried = None
+        if stop < EXT - SKIP:
+            carried = driving(step, comp, stop, 8)
         for base in reversed(range(start, stop, n)):
-            at, nxt = pl.ds(base, n), pl.ds(base + 1, n)
-            row = lax.broadcasted_iota(jnp.int32, (n, LANES), 0) + base
-            lane = lane_of((n, LANES))
-            inside = (row >= lo) & (row < hi)
-            held = [inside & has_left, inside, inside, inside & has_right]
-            v = [v_ref[k, at, :] for k in range(4)]
-            if True:
-                out = []
-                for k in range(4):
-                    if step == 0:
-                        w = w_ref[comp, k, at, :]
-                    else:
-                        w = r_ref[comp, k, at, :] * c_ref[comp, k, at, :]
-                    if comp == 0:
-                        beside = v_ref[k, nxt, :]
-                    else:
-                        beside = roll(jnp.where(lane == 0, v[min(k + 1, 3)], v[k]), LANES - 1)
-                    out.append(jnp.where(held[k], v[k] - beside - w, 0.0))
-                nexts = []
-                for k in range(4):
-                    after = carried.get((comp, k), out[k][0:8])
-                    nexts.append(pltpu.roll(jnp.concatenate([out[k], after], axis=0), n + 7, 0)[0:n])
-                    carried[comp, k] = out[k][0:8]
-                for k, value in windows(out, nexts, blocks_of(step, comp)).items():
-                    for g in range(n // 8):
-                        spot = pl.ds((base - SKIP) // 8 + g, 8, stride=PITCH)
-                        drive_ref[10 * comp + k + 1, spot, :] = value[8 * g : 8 * g + 8]
+            size = min(n, stop - base)
+            out = driving(step, comp, base, size)
+            nexts = []
+            for k in range(4):
+                after = out[k][0:8] if carried is None else carried[k]
+                nexts.append(pltpu.roll(jnp.concatenate([out[k], after], axis=0), size + 7, 0)[0:size])
+            carried = [one[0:8] for one in out]
+            for k, value in windows(out, nexts, blocks_of(step, comp)).items():
+                for g in range(size // 8):
+                    spot = pl.ds((base - SKIP) // 8 + g, 8, stride=PITCH)
+                    drive_ref[10 * comp + k + 1, spot, :] = value[8 * g : 8 * g + 8]
 
     def blocks_of(step, comp):
         if step == 0:
@@ -346,18 +355,26 @@
                 for side in range(2):
                     part[side][k] = product[i * n : (i + 1) * n, side * LANES : (side + 1) * LANES]
         lane = lane_of((n, LANES))
+
+        def chosen(options):
+            value = None
+            for group in reversed(range(4)):
+                if options[group] is not None:
+                    value = options[group] if value is None else jnp.where(lane < STRIP * (group + 1), options[group], value)
+            return value
+
         for side in range(2):
-            for t in range(4):
-                for tile in range(4):
-                    value = None
-                    for q in reversed(range(4)):
-                        k = 4 * (tile - 1) + q
-                        if k in part[side]:
-                            turn = (q - t) % 4
-                            piece = roll(part[side][k], STRIP * turn) if turn else part[side][k]
-                            value = piece if value is None else jnp.where(lane < STRIP * (q + 1), piece, value)
-                    if value is not None:
-                        flow_ref[comp, tile, pl.ds((4 * side + t) * FLOW + start // 8, n), :] = value
+            for tile in range(4):
+                held = [part[side].get(4 * (tile - 1) + q) for q in range(4)]
+                if all(one is None for one in held):
+                    continue
+                moved = []
+                for d in range(4):
+                    value = chosen([held[(t + d) % 4] for t in range(4)])
+                    moved.append(roll(value, STRIP * d) if d else value)
+                for t in range(4):
+                    value = chosen([None if held[q] is None else moved[(q - t) % 4] for q in range(4)])
+                    flow_ref[comp, tile, pl.ds((4 * side + t) * FLOW + start // 8, n), :] = value
 
     def flow(comp, tile, first, n):
         parts = [flow_ref[comp, tile, pl.ds(first // 8 + g, 8, stride=FLOW), :] for g in range(n // 8)]
@@ -428,19 +445,32 @@
         def _(which=which):
             message(which).start()
     build_table(k_ref, pad_ref, base_ref, table_ref)
-    for which, (dr, dc) in enumerate(DIRECTIONS):
-        @pl.when(exists(-dr, -dc))
-        def _(which=which):
-            message(which).wait_recv()
-    unpack_sides()
+    def receive(wanted):
+        for which in wanted:
+            dr, dc = DIRECTIONS[which]
+
+            @pl.when(exists(-dr, -dc))
+            def _(which=which):
+                message(which).wait_recv()
+
+    low, high = TOP, TOP + ROWS
+    receive((0, 1))
     unpack_ends()
+    receive((2, 3))
+    unpack_sides(low, high, 16)
     for comp in range(2):
-        drive(0, comp)
+        drive(0, comp, low, high - 16)
+    receive((4, 5, 6, 7))
+    unpack_sides(SKIP, low, 8)
+    unpack_sides(high, EXT - SKIP, 8)
+    for comp in range(2):
+        drive(0, comp, high - 16, EXT - SKIP)
+        drive(0, comp, SKIP, low)
         convolve(0, comp)
     advance_frame()
     update_frame()
     for comp in range(2):
-        drive(1, comp)
+        drive(1, comp, FROM, EXT - FROM)
         convolve(1, comp)
     finish()
     for which, (dr, dc) in enumerate(DIRECTIONS):
@@ -495,7 +525,23 @@
     held = [waveforms, jnp.transpose(k_window, (1, 0, 2)), voltage, currents, resistance, inverse_cap]
     held += [shunt_conductance, tap_index, pad_mask]
     held = [pltpu.with_memory_space_constraint(one, pltpu.HBM) for one in held]
-    return call(*held)
+    voltage_new, currents_new = call(*held)
+
+    def copy_out(v_ref, c_ref, vout_hbm, cout_hbm, sem):
+        copies = [pltpu.make_async_copy(v_ref, vout_hbm, sem.at[0]), pltpu.make_async_copy(c_ref, cout_hbm, sem.at[1])]
+        for one in copies:
+            one.start()
+        for one in copies:
+            one.wait()
+
+    return pl.pallas_call(
+        copy_out,
+        out_shape=(jax.ShapeDtypeStruct(block, F32), jax.ShapeDtypeStruct((2, *block), F32)),
+        in_specs=[vmem, vmem],
+        out_specs=(hbm, hbm),
+        scratch_shapes=[pltpu.SemaphoreType.DMA((2,))],
+        compiler_params=pltpu.CompilerParams(vmem_limit_bytes=1024 * 1024),
+    )(voltage_new, currents_new)
 
 
 def solution(mesh):

time: 14.8 us -> 13.8 us (0.932)
  local copies, waits for them, and re-layouts: 1.36 us -> 0 us
  Pallas kernels: 12.6 us -> 13 us
    unnamed x2 -> x0, local copies, waits for them, and re-layouts: 1.36 us -> none
    pallas_call x1 -> x2, Pallas kernels: 12.6 us -> 13 us  [the longest x1 12.2 us: local(): voltage_new, currents_new = call(*held)]
where the time goes in v4:
time: 13.8 us; the launch traced here: 13.6 us
  Pallas kernels  13 us (94%)
  between operations  0.64 us (5%)
    pallas_call x1, Pallas kernels, local(): voltage_new, currents_new = call(*held)  12.2 us
    pallas_call x1, Pallas kernels, local(): pl.pallas_call(copy_out, out_shape=(jax.ShapeDtypeStruct(block, F32), jax...  0.77 us

profile of v4, /device:TPU:97, one launch (start us, length us, event | category | flops | bytes accessed | tf_op | source)
XLA Modules:
  0.0 13.6 jit_solution(1923156160604039084)
XLA Ops:
  0.6 12.2 %shard_map.104 = (f32[128,256]{1,0:T(8,128)S(1)}, f32[2,128,256]{2,1,0:T(8,128)S(1)}) custom-call(f32[2,8]{1,0:T(2,128)} %wave_hbm.1, bf16[33,2,33]{2,1,0:T(2,128)(2,1)} %bitcast.1, f32[128,256]{1,0:T(8,128)} %v_hbm.1, f32[2,128,256]{2,1,0:T(8,128)} %c_hbm.1, f32[2,128,256]{2,1,0:T(8,128)} %r_hbm.1, f32[128,256]{1,0:T(8,128)} %cap_hbm.1, ...), custom_call_target="tpu_custom_call" | custom-call | tf_op jit(solution)/shard_map/pallas_call | solution.py:528
  12.9 0.8 %shard_map.105 = (f32[128,256]{1,0:T(8,128)}, f32[2,128,256]{2,1,0:T(8,128)}) custom-call(f32[128,256]{1,0:T(8,128)S(1)} %get-tuple-element.4.v_ref, f32[2,128,256]{2,1,0:T(8,128)S(1)} %get-tuple-element.5.c_ref), custom_call_target="tpu_custom_call" | custom-call | tf_op jit(solution)/shard_map/pallas_call | solution.py:537
